TPU v7x, 32 devices: a whole 2x2x4 slice. The times are simulated.
32 devices in a mesh: shard: 2 (over x), replica: 16 (over z, y, core).
Axes of the slice: x: 2, y: 2, z: 4, core: 2. Of those that a mesh axis runs over, the one named last changes fastest.
Arguments:
- hidden_in: bfloat16 [16384, 2048], P(('shard', 'replica')), may hold values from -6 to 6
- out_cotangent: bfloat16 [16384, 2048], P(('shard', 'replica')), may hold values from -6 to 6
- segment_ids: int32 [16384], P(('shard', 'replica')), may hold values from 0 to 124, as said below
- ln1_gain: bfloat16 [2048], P('shard'), may hold values from 0.5 to 1.5
- ln1_bias: bfloat16 [2048], P('shard'), may hold values from -3 to 3
- qkv_weight: bfloat16 [2048, 6144], P('shard'), may hold values from -0.125 to 0.125
- qkv_bias: bfloat16 [6144], P('shard'), may hold values from -3 to 3
- dense_weight: bfloat16 [2048, 2048], P('shard'), may hold values from -0.375 to 0.375
- dense_bias: bfloat16 [2048], P('shard'), may hold values from -3 to 3
- ln2_gain: bfloat16 [2048], P('shard'), may hold values from 0.5 to 1.5
- ln2_bias: bfloat16 [2048], P('shard'), may hold values from -3 to 3
- fc1_weight: bfloat16 [2048, 4096], P('shard'), may hold values from -0.125 to 0.125
- fc1_bias: bfloat16 [4096], P('shard'), may hold values from -3 to 3
- fc2_weight: bfloat16 [4096, 2048], P('shard'), may hold values from -0.125 to 0.125
- fc2_bias: bfloat16 [2048], P('shard'), may hold values from -3 to 3
Outputs:
- hidden_out: bfloat16 [16384, 2048], P(('shard', 'replica'))
- grad_input: float32 [16384, 2048], P(('shard', 'replica'))
- grad_ln1_gain: float32 [2048], P(('shard', 'replica'))
- grad_ln1_bias: float32 [2048], P(('shard', 'replica'))
- grad_qkv_weight: float32 [2048, 6144], P(('shard', 'replica'))
- grad_qkv_bias: float32 [6144], P(('shard', 'replica'))
- grad_dense_weight: float32 [2048, 2048], P(('shard', 'replica'))
- grad_dense_bias: float32 [2048], P(('shard', 'replica'))
- grad_ln2_gain: float32 [2048], P(('shard', 'replica'))
- grad_ln2_bias: float32 [2048], P(('shard', 'replica'))
- grad_fc1_weight: float32 [2048, 4096], P(('shard', 'replica'))
- grad_fc1_bias: float32 [4096], P(('shard', 'replica'))
- grad_fc2_weight: float32 [4096, 2048], P(('shard', 'replica'))
- grad_fc2_bias: float32 [2048], P(('shard', 'replica'))
Inputs may be any that keep to these rules, and one draw needn't show every extreme that they name: `segment_ids`: segment ids start at 0 and rise by one at each new sequence along the tokens; a segment lies within one aligned run of 512 tokens, so within one block of 512 tokens, and has at most 512 tokens; some block consists of segments of exactly 512 tokens.
All inputs are finite; a program needn't handle non-finite values.
Results may differ from a plain program's by a relative error of at most 0.0094.
Values may be sent and summed in bfloat16 or wider, within the bound.
A program may use at most 448 MiB of HBM per device.

v0:
```python
from functools import partial

import jax
import jax.numpy as jnp
from jax import lax
from jax.sharding import PartitionSpec as P

HEADS = 8
HEAD = 256
ROT = 64


NEG_FILL = -1e30
EPSILON = 1e-05


def layer_norm(values, gain_w, bias_w):
    center = values - jnp.mean(values, axis=-1, keepdims=True)
    spread = jnp.mean(center * center, axis=-1, keepdims=True)
    return center * lax.rsqrt(spread + EPSILON) * gain_w + bias_w


def rotary_angles(seg_row):
    row_count = seg_row.shape[0]
    row_index = jnp.arange(row_count, dtype=jnp.int32)
    same_seg = seg_row[:, None] == seg_row[None, :]
    first_pos = jnp.min(jnp.where(same_seg, row_index[None, :], row_count), axis=1)
    offset = (row_index - first_pos).astype(jnp.float32)
    frequency = jnp.exp(-jnp.log(10000.0) * jnp.arange(0, ROT, 2).astype(jnp.float32) / ROT)
    angles = offset[:, None] * frequency[None, :]
    allowed = same_seg & (row_index[None, :] <= row_index[:, None])
    return (jnp.cos(angles), jnp.sin(angles), allowed)


def rotate(heads_in, cos_table, sin_table):
    half_rot = ROT // 2
    part_one = heads_in[..., :half_rot]
    part_two = heads_in[..., half_rot:ROT]
    cos_b = cos_table[:, None, :]
    sin_b = sin_table[:, None, :]
    return jnp.concatenate(
        [
            part_one * cos_b - part_two * sin_b,
            part_two * cos_b + part_one * sin_b,
            heads_in[..., ROT:],
        ],
        axis=-1,
    )


def gelu_exact(values):
    return 0.5 * values * (1.0 + lax.erf(values * 0.7071067811865476))


def masked_scores(query_b, keys_b, allowed):
    inv_root = query_b.shape[-1] ** (-0.5)
    scores = (
        jnp.einsum("qhd,khd->hqk", query_b, keys_b, preferred_element_type=jnp.float32) * inv_root
    )
    return jnp.where(allowed[None], scores, NEG_FILL)


def attention_forward(query_b, keys_b, vals_b, allowed):
    scores = masked_scores(query_b, keys_b, allowed)
    row_peak = jnp.max(scores, axis=-1, keepdims=True)
    exp_terms = jnp.exp(scores - row_peak)
    row_total = jnp.sum(exp_terms, axis=-1, keepdims=True)
    log_total = (row_peak + jnp.log(row_total))[..., 0]
    probs_b = (exp_terms / row_total).astype(jnp.bfloat16)
    context = jnp.einsum("hqk,khd->qhd", probs_b, vals_b, preferred_element_type=jnp.float32)
    return (context, log_total)


def attention_backward(query_b, keys_b, vals_b, allowed, log_total, context, grad_ctx):
    inv_root = query_b.shape[-1] ** (-0.5)
    scores = masked_scores(query_b, keys_b, allowed)
    probs_f = jnp.exp(scores - log_total[..., None])
    probs_fb = probs_f.astype(jnp.bfloat16)
    grad_probs = jnp.einsum("qhd,khd->hqk", grad_ctx, vals_b, preferred_element_type=jnp.float32)
    grad_vals = jnp.einsum("hqk,qhd->khd", probs_fb, grad_ctx, preferred_element_type=jnp.float32)
    row_dot = jnp.sum(grad_ctx.astype(jnp.float32) * context, axis=-1).T
    grad_scores = (probs_f * (grad_probs - row_dot[:, :, None]) * inv_root).astype(jnp.bfloat16)
    grad_query = jnp.einsum("hqk,khd->qhd", grad_scores, keys_b, preferred_element_type=jnp.float32)
    grad_keys = jnp.einsum("hqk,qhd->khd", grad_scores, query_b, preferred_element_type=jnp.float32)
    return (grad_query, grad_keys, grad_vals)


def local(
    hidden_in,
    out_cotangent,
    segment_ids,
    ln1_gain,
    ln1_bias,
    qkv_weight,
    qkv_bias,
    dense_weight,
    dense_bias,
    ln2_gain,
    ln2_bias,
    fc1_weight,
    fc1_bias,
    fc2_weight,
    fc2_bias,
):
    attn_full = (
        lax.all_gather(ln1_gain, "shard", axis=0, tiled=True),
        lax.all_gather(ln1_bias, "shard", axis=0, tiled=True),
        lax.all_gather(qkv_weight, "shard", axis=0, tiled=True),
        lax.all_gather(qkv_bias, "shard", axis=0, tiled=True),
        lax.all_gather(dense_weight, "shard", axis=0, tiled=True),
        lax.all_gather(dense_bias, "shard", axis=0, tiled=True),
    )
    row_count, model_width = hidden_in.shape
    inputs_f = hidden_in.astype(jnp.float32)
    cos_table, sin_table, allowed = rotary_angles(segment_ids)
    gain_one_f = attn_full[0].astype(jnp.float32)
    bias_one_f = attn_full[1].astype(jnp.float32)
    normed_one = layer_norm(inputs_f, gain_one_f, bias_one_f).astype(jnp.bfloat16)
    packed = jnp.dot(normed_one, attn_full[2], preferred_element_type=jnp.float32) + attn_full[
        3
    ].astype(jnp.float32)
    query_pre = packed[:, :model_width].reshape(row_count, HEADS, HEAD)
    keys_pre = packed[:, model_width : 2 * model_width].reshape(row_count, HEADS, HEAD)
    query_b = rotate(query_pre, cos_table, sin_table).astype(jnp.bfloat16)
    keys_b = rotate(keys_pre, cos_table, sin_table).astype(jnp.bfloat16)
    vals_b = packed[:, 2 * model_width :].reshape(row_count, HEADS, HEAD).astype(jnp.bfloat16)
    context, log_total = attention_forward(query_b, keys_b, vals_b, allowed)
    context_b = context.reshape(row_count, model_width).astype(jnp.bfloat16)
    attn_out = jnp.dot(context_b, attn_full[4], preferred_element_type=jnp.float32) + attn_full[
        5
    ].astype(jnp.float32)
    mlp_full = (
        lax.all_gather(ln2_gain, "shard", axis=0, tiled=True),
        lax.all_gather(ln2_bias, "shard", axis=0, tiled=True),
        lax.all_gather(fc1_weight, "shard", axis=0, tiled=True),
        lax.all_gather(fc1_bias, "shard", axis=0, tiled=True),
        lax.all_gather(fc2_weight, "shard", axis=0, tiled=True),
        lax.all_gather(fc2_bias, "shard", axis=0, tiled=True),
    )
    gain_two_f = mlp_full[0].astype(jnp.float32)
    bias_two_f = mlp_full[1].astype(jnp.float32)
    normed_two = layer_norm(inputs_f, gain_two_f, bias_two_f).astype(jnp.bfloat16)
    pre_act = jnp.dot(normed_two, mlp_full[2], preferred_element_type=jnp.float32) + mlp_full[
        3
    ].astype(jnp.float32)
    act_b = gelu_exact(pre_act).astype(jnp.bfloat16)
    mlp_out = jnp.dot(act_b, mlp_full[4], preferred_element_type=jnp.float32) + mlp_full[5].astype(
        jnp.float32
    )
    result = (inputs_f + attn_out + mlp_out).astype(jnp.bfloat16)
    mlp_back = (
        lax.all_gather(ln2_gain, "shard", axis=0, tiled=True),
        lax.all_gather(ln2_bias, "shard", axis=0, tiled=True),
        lax.all_gather(fc1_weight, "shard", axis=0, tiled=True),
        lax.all_gather(fc1_bias, "shard", axis=0, tiled=True),
        lax.all_gather(fc2_weight, "shard", axis=0, tiled=True),
        lax.all_gather(fc2_bias, "shard", axis=0, tiled=True),
    )
    cot_f = out_cotangent.astype(jnp.float32)
    grad_w_down = jnp.einsum("tf,td->fd", act_b, out_cotangent, preferred_element_type=jnp.float32)
    grad_b_down = jnp.sum(cot_f, axis=0)
    grad_act = jnp.einsum(
        "td,fd->tf", out_cotangent, mlp_back[4], preferred_element_type=jnp.float32
    )
    grad_pre = jax.vjp(gelu_exact, pre_act)[1](grad_act)[0]
    grad_pre_b = grad_pre.astype(jnp.bfloat16)
    grad_w_up = jnp.einsum("td,tf->df", normed_two, grad_pre_b, preferred_element_type=jnp.float32)
    grad_b_up = jnp.sum(grad_pre, axis=0)
    grad_normed_two = jnp.einsum(
        "tf,df->td", grad_pre_b, mlp_back[2], preferred_element_type=jnp.float32
    )
    norm_back_two = jax.vjp(
        layer_norm, inputs_f, mlp_back[0].astype(jnp.float32), mlp_back[1].astype(jnp.float32)
    )[1]
    grad_in_two, grad_gain_two, grad_bias_two = norm_back_two(grad_normed_two)
    mlp_parts = (
        lax.psum_scatter(grad_gain_two, ("shard", "replica"), scatter_dimension=0, tiled=True),
        lax.psum_scatter(grad_bias_two, ("shard", "replica"), scatter_dimension=0, tiled=True),
        lax.psum_scatter(grad_w_up, ("shard", "replica"), scatter_dimension=0, tiled=True),
        lax.psum_scatter(grad_b_up, ("shard", "replica"), scatter_dimension=0, tiled=True),
        lax.psum_scatter(grad_w_down, ("shard", "replica"), scatter_dimension=0, tiled=True),
        lax.psum_scatter(grad_b_down, ("shard", "replica"), scatter_dimension=0, tiled=True),
    )
    attn_back = (
        lax.all_gather(ln1_gain, "shard", axis=0, tiled=True),
        lax.all_gather(ln1_bias, "shard", axis=0, tiled=True),
        lax.all_gather(qkv_weight, "shard", axis=0, tiled=True),
        lax.all_gather(qkv_bias, "shard", axis=0, tiled=True),
        lax.all_gather(dense_weight, "shard", axis=0, tiled=True),
        lax.all_gather(dense_bias, "shard", axis=0, tiled=True),
    )
    grad_w_dense = jnp.einsum(
        "td,te->de", context_b, out_cotangent, preferred_element_type=jnp.float32
    )
    grad_b_dense = jnp.sum(cot_f, axis=0)
    grad_ctx = (
        jnp.einsum("te,de->td", out_cotangent, attn_back[4], preferred_element_type=jnp.float32)
        .astype(jnp.bfloat16)
        .reshape(row_count, HEADS, HEAD)
    )
    grad_query, grad_keys, grad_vals = attention_backward(
        query_b, keys_b, vals_b, allowed, log_total, context, grad_ctx
    )
    rotate_back = jax.vjp(partial(rotate, cos_table=cos_table, sin_table=sin_table), query_pre)[1]
    grad_query_pre = rotate_back(grad_query)[0]
    grad_keys_pre = rotate_back(grad_keys)[0]
    grad_packed = jnp.concatenate(
        [
            grad_query_pre.reshape(row_count, model_width),
            grad_keys_pre.reshape(row_count, model_width),
            grad_vals.reshape(row_count, model_width),
        ],
        axis=1,
    )
    grad_packed_b = grad_packed.astype(jnp.bfloat16)
    grad_w_qkv = jnp.einsum(
        "td,tf->df", normed_one, grad_packed_b, preferred_element_type=jnp.float32
    )
    grad_b_qkv = jnp.sum(grad_packed, axis=0)
    grad_normed_one = jnp.einsum(
        "tf,df->td", grad_packed_b, attn_back[2], preferred_element_type=jnp.float32
    )
    norm_back_one = jax.vjp(
        layer_norm, inputs_f, attn_back[0].astype(jnp.float32), attn_back[1].astype(jnp.float32)
    )[1]
    grad_in_one, grad_gain_one, grad_bias_one = norm_back_one(grad_normed_one)
    grad_rows = cot_f + grad_in_one + grad_in_two
    attn_parts = (
        lax.psum_scatter(grad_gain_one, ("shard", "replica"), scatter_dimension=0, tiled=True),
        lax.psum_scatter(grad_bias_one, ("shard", "replica"), scatter_dimension=0, tiled=True),
        lax.psum_scatter(grad_w_qkv, ("shard", "replica"), scatter_dimension=0, tiled=True),
        lax.psum_scatter(grad_b_qkv, ("shard", "replica"), scatter_dimension=0, tiled=True),
        lax.psum_scatter(grad_w_dense, ("shard", "replica"), scatter_dimension=0, tiled=True),
        lax.psum_scatter(grad_b_dense, ("shard", "replica"), scatter_dimension=0, tiled=True),
    )
    every_part = tuple(attn_parts) + tuple(mlp_parts)
    return (
        result,
        grad_rows,
        every_part[0],
        every_part[1],
        every_part[2],
        every_part[3],
        every_part[4],
        every_part[5],
        every_part[6],
        every_part[7],
        every_part[8],
        every_part[9],
        every_part[10],
        every_part[11],
    )


def solution(mesh):
    return jax.shard_map(
        local,
        mesh=mesh,
        in_specs=(
            P(("shard", "replica"), None),
            P(("shard", "replica"), None),
            P(("shard", "replica")),
            P("shard"),
            P("shard"),
            P("shard", None),
            P("shard"),
            P("shard", None),
            P("shard"),
            P("shard"),
            P("shard"),
            P("shard", None),
            P("shard"),
            P("shard", None),
            P("shard"),
        ),
        out_specs=(
            P(("shard", "replica"), None),
            P(("shard", "replica"), None),
            P(("shard", "replica")),
            P(("shard", "replica")),
            P(("shard", "replica"), None),
            P(("shard", "replica")),
            P(("shard", "replica"), None),
            P(("shard", "replica")),
            P(("shard", "replica")),
            P(("shard", "replica")),
            P(("shard", "replica"), None),
            P(("shard", "replica")),
            P(("shard", "replica"), None),
            P(("shard", "replica")),
        ),
        check_vma=False,
    )
```

profile of v0, /device:TPU:0, one launch (start us, length us, event | category | flops | bytes accessed | tf_op | source)
XLA Modules:
  0.0 2444.1 jit_solution(16074409329051763728)
XLA Ops:
  41.9 74.5 %all-gather.7.cloned.1.call-done = bf16[2048,2048]{1,0:T(8,128)(2,1)} async-done(((bf16[1024,2048]{1,0:T(8,128)(2,1)}), bf16[2048,2048]{1,0:T(8,128)(2,1)}) %all-gather.7.cloned.1.call-update) | async-done | bytes 8388624 | tf_op jit(solution)/shard_map/all_gather | solution.py:110
  116.4 9.9 convolution_convert_fusion
  130.7 186.1 %all-gather.9.cloned.1.call-done = bf16[2048,4096]{1,0:T(8,128)(2,1)} async-done(((bf16[1024,4096]{1,0:T(8,128)(2,1)}), bf16[2048,4096]{1,0:T(8,128)(2,1)}) %all-gather.9.cloned.1.call-update) | async-done | bytes 16777232 | tf_op jit(solution)/shard_map/all_gather | solution.py:135
  316.8 15.1 fusion.56
  331.9 185.4 %all-gather.11.cloned.1.call-done = bf16[4096,2048]{1,0:T(8,128)(2,1)} async-done(((bf16[2048,2048]{1,0:T(8,128)(2,1)}), bf16[4096,2048]{1,0:T(8,128)(2,1)}) %all-gather.11.cloned.1.call-update) | async-done | bytes 16777232 | tf_op jit(solution)/shard_map/all_gather | solution.py:137
  517.3 19.5 fusion.65
  536.8 16.6 fusion.40
  553.4 258.9 %all-gather.5.cloned.1.call-done = bf16[2048,6144]{1,0:T(8,128)(2,1)} async-done(((bf16[1024,6144]{1,0:T(8,128)(2,1)}), bf16[2048,6144]{1,0:T(8,128)(2,1)}) %all-gather.5.cloned.1.call-update) | async-done | bytes 25165840 | tf_op jit(solution)/shard_map/all_gather | solution.py:108
  812.4 21.0 convolution_add_fusion
  891.4 8.0 fusion.27
  909.3 7.6 pad_add_fusion
  922.2 7.4 fusion
  929.6 23.5 fusion.64
  965.3 12.5 fusion.70
  978.5 17.8 fusion.38
  997.0 18.2 fusion.62
  1016.0 24.6 %fusion.51 = f32[2048,6144]{1,0:T(8,128)} fusion(f32[512,2048]{0,1:T(8,128)} %bitcast.70, f32[512,2048]{0,1:T(8,128)} %bitcast.63, f32[512,2048]{0,1:T(8,128)} %bitcast.60, bf16[512,2048]{1,0:T(8,128)(2,1)S(1)} %copy-done, f32[2048]{0:T(1024)S(1)} %copy-done.24, f32[2048]{0:T(1024)S(1)} %convert_element_type.92, f32[512]{0:T(512)S(1)} %fusion.45, ...), kind=kOutput, calls=%fused_computation.102 | convolution fusion | flops 12910067712 | bytes 65032192 | tf_op jit(solution)/shard_map/td,tf->df/dot_general | solution.py:216
  1050.2 7.6 fusion.69
  1057.9 17.2 fusion.26
  1075.1 15.6 all-reduce.16.cloned.1.call-done
  1099.0 179.0 %reduce-scatter.7.cloned.1.call-done = f32[64,2048]{1,0:T(8,128)} async-done(((f32[2048,2048]{1,0:T(8,128)}), f32[64,2048]{1,0:T(8,128)}) %reduce-scatter.7.cloned.1.call-update) | async-done | bytes 524304 | tf_op jit(solution)/shard_map/reduce_scatter | solution.py:233
  1278.0 358.6 %reduce-scatter.9.cloned.1.call-done = f32[64,4096]{1,0:T(8,128)} async-done(((f32[2048,4096]{1,0:T(8,128)}), f32[64,4096]{1,0:T(8,128)}) %reduce-scatter.9.cloned.1.call-update) | async-done | bytes 1048592 | tf_op jit(solution)/shard_map/reduce_scatter | solution.py:179
  1636.6 360.5 %reduce-scatter.11.cloned.1.call-done = f32[128,2048]{1,0:T(8,128)} async-done(((f32[4096,2048]{1,0:T(8,128)}), f32[128,2048]{1,0:T(8,128)}) %reduce-scatter.11.cloned.1.call-update) | async-done | bytes 1048592 | tf_op jit(solution)/shard_map/reduce_scatter | solution.py:181
  1997.1 439.7 %reduce-scatter.5.cloned.1.call-done = f32[64,6144]{1,0:T(8,128)} async-done(((f32[2048,6144]{1,0:T(8,128)}), f32[64,6144]{1,0:T(8,128)}) %reduce-scatter.5.cloned.1.call-update) | async-done | bytes 1572880 | tf_op jit(solution)/shard_map/reduce_scatter | solution.py:231
  (153 shorter events, 144.8 us)
Async XLA Ops:
  7.2 109.2 %all-gather.7.cloned.1.call-start = ((), (), s32[]{:S(2)}) async-start(), calls=%async_computation.5 | async-start | bytes 12582912 | tf_op jit(solution)/shard_map/all_gather | solution.py:110
  7.9 308.9 %all-gather.9.cloned.1.call-start = ((), (), s32[]{:S(2)}) async-start(), calls=%async_computation.6 | async-start | bytes 25165824 | tf_op jit(solution)/shard_map/all_gather | solution.py:135
  8.7 508.6 %all-gather.11.cloned.1.call-start = ((), (), s32[]{:S(2)}) async-start(), calls=%async_computation.7 | async-start | bytes 25165824 | tf_op jit(solution)/shard_map/all_gather | solution.py:137
  9.4 10.5 copy-start.27
  9.4 14.9 copy-start.31
  9.4 19.4 copy-start.32
  9.4 23.9 copy-start.28
  9.5 28.5 %copy-start.18 = (s32[512]{0:T(512)S(1)}, s32[512]{0:T(512)}, u32[]{:S(2)}) copy-start(s32[512]{0:T(512)} %param.17) | copy-start | bytes 6148
  9.5 28.7 %copy-start = (bf16[512,2048]{1,0:T(8,128)(2,1)S(1)}, bf16[512,2048]{1,0:T(8,128)(2,1)}, u32[]{:S(2)}) copy-start(bf16[512,2048]{1,0:T(8,128)(2,1)} %param.15) | copy-start | bytes 6291460
  9.5 802.9 %all-gather.5.cloned.1.call-start = ((), (), s32[]{:S(2)}) async-start(), calls=%async_computation.4 | async-start | bytes 37748736 | tf_op jit(solution)/shard_map/all_gather | solution.py:108
  10.1 1080.6 %all-reduce.16.cloned.1.call-start = ((), (), s32[]{:S(2)}) async-start(), calls=%async_computation.12 | async-start | bytes 163840
  19.9 792.5 %copy-start.23 = (f32[2048]{0:T(1024)}, f32[2048]{0:T(1024)S(1)}, u32[]{:S(2)}) copy-start(f32[2048]{0:T(1024)S(1)} %convert_element_type.93) | copy-start | bytes 24580
  28.8 288.0 %copy-start.16 = (f32[2048]{0:T(1024)}, f32[2048]{0:T(1024)S(1)}, u32[]{:S(2)}) copy-start(f32[2048]{0:T(1024)S(1)} %convert_element_type.103) | copy-start | bytes 24580
  33.4 283.5 %copy-start.25 = (f32[2048]{0:T(1024)}, f32[2048]{0:T(1024)S(1)}, u32[]{:S(2)}) copy-start(f32[2048]{0:T(1024)S(1)} %convert_element_type.104) | copy-start | bytes 24580
  38.0 479.3 %copy-start.21 = (f32[4096]{0:T(1024)}, f32[4096]{0:T(1024)S(1)}, u32[]{:S(2)}) copy-start(f32[4096]{0:T(1024)S(1)} %convert_element_type.106) | copy-start | bytes 49156
  39.3 87.0 %copy-start.19 = (f32[512]{0:T(512)}, f32[512]{0:T(512)S(1)}, u32[]{:S(2)}) copy-start(f32[512]{0:T(512)S(1)} %fusion.22) | copy-start | bytes 6148
  862.3 8.0 copy-start.4
  891.4 8.0 copy-start.5
  929.6 23.5 copy-start.20
  964.8 313.2 %reduce-scatter.7.cloned.1.call-start = ((), (), s32[]{:S(2)}) async-start(), calls=%async_computation.9 | async-start | bytes 17301504 | tf_op jit(solution)/shard_map/reduce_scatter | solution.py:233
  977.8 658.8 %reduce-scatter.9.cloned.1.call-start = ((), (), s32[]{:S(2)}) async-start(), calls=%async_computation.10 | async-start | bytes 34603008 | tf_op jit(solution)/shard_map/reduce_scatter | solution.py:179
  996.3 1000.8 %reduce-scatter.11.cloned.1.call-start = ((), (), s32[]{:S(2)}) async-start(), calls=%async_computation.11 | async-start | bytes 34603008 | tf_op jit(solution)/shard_map/reduce_scatter | solution.py:181
  1015.3 1421.5 %reduce-scatter.5.cloned.1.call-start = ((), (), s32[]{:S(2)}) async-start(), calls=%async_computation.8 | async-start | bytes 51904512 | tf_op jit(solution)/shard_map/reduce_scatter | solution.py:231
  1091.4 1346.0 %copy-start.35 = (f32[64]{0:T(128)}, f32[64]{0:T(128)S(1)}, u32[]{:S(2)}) copy-start(f32[64]{0:T(128)S(1)} %dynamic-slice.3) | copy-start | bytes 772
  (21 other events, 81.2 us)
Sparse Core Ops, SparseCore 0:
  9.5 106.8 all-gather.6
  118.0 198.8 all-gather.8
  318.4 198.8 all-gather.10
  518.7 293.6 all-gather.4
  965.0 125.6 all-reduce.15
  1093.4 184.5 reduce-scatter.6
  1280.9 355.7 reduce-scatter.8
  1639.5 357.5 reduce-scatter.10
  2004.1 432.6 reduce-scatter.4
where the time goes:
time: 2450 us; the launch traced here: 2440 us
  waiting for transfers between devices  2060 us (84%)
  matrix products  235 us (10%)
  local copies, waits for them, and re-layouts  51.9 us (2%)
  other arithmetic  44.3 us (2%)
  blocking collectives  36.7 us (1%)
    reduce_scatter x1, waiting for transfers between devices, local(): lax.psum_scatter(grad_w_qkv, ('shard', 'replica'), scatter_dimension=0, t...  440 us
    reduce_scatter x1, waiting for transfers between devices, local(): lax.psum_scatter(grad_w_down, ('shard', 'replica'), scatter_dimension=0,...  361 us
    reduce_scatter x1, waiting for transfers between devices, local(): lax.psum_scatter(grad_w_up, ('shard', 'replica'), scatter_dimension=0, ti...  359 us
    all_gather x1, waiting for transfers between devices, local(): lax.all_gather(qkv_weight, 'shard', axis=0, tiled=True)  259 us
    all_gather x1, waiting for transfers between devices, local(): lax.all_gather(fc1_weight, 'shard', axis=0, tiled=True)  186 us
    all_gather x1, waiting for transfers between devices, local(): lax.all_gather(fc2_weight, 'shard', axis=0, tiled=True)  185 us
    reduce_scatter x1, waiting for transfers between devices, local(): lax.psum_scatter(grad_w_dense, ('shard', 'replica'), scatter_dimension=0,...  179 us
    all_gather x1, waiting for transfers between devices, local(): lax.all_gather(dense_weight, 'shard', axis=0, tiled=True)  74.5 us
  transfers between devices with their start and end apart: 9, of which 9 were waited for; matrix products, arithmetic and copies ran while one was open for 7% of the time, Pallas kernels for 0%

commit v1 on v0

v1 whole, which is shorter than its diff:
```python
from functools import partial

import jax
import jax.numpy as jnp
from jax import lax
from jax.experimental import pallas as pl
from jax.experimental.pallas import tpu as pltpu
from jax.sharding import PartitionSpec as P

HEADS = 8
HEAD = 256
ROT = 64
NEG_FILL = -1e30
EPSILON = 1e-05
BF = jnp.bfloat16
F32 = jnp.float32
MESH = pl.DeviceIdType.MESH
ANY = pl.BlockSpec(memory_space=pl.ANY)
VMEM_LIMIT = 62 << 20


def dot(a, b, da, db):
    return lax.dot_general(a, b, (((da,), (db,)), ((), ())), preferred_element_type=F32)


def flat(v):
    return v.reshape((-1, v.shape[-1]))


class Place:
    def __init__(self, nbits):
        self.nbits = nbits
        self.s = lax.axis_index("shard")
        self.rep = lax.axis_index("replica")
        self.c = self.rep % 2
        self.r = self.rep // 2
        self.bits = [(self.r // 2 ** (nbits - 1 - b)) % 2 for b in range(nbits)]
        self.over_x = (1 - self.s, self.rep)
        self.over_core = (self.s, self.rep + 1 - 2 * self.c)
        self.diagonal = (1 - self.s, self.rep + 1 - 2 * self.c)

    def over_bit(self, b):
        return (self.s, self.rep + (1 - 2 * self.bits[b]) * 2 ** (self.nbits - b))

    def peers(self):
        return [self.over_x, self.over_core, self.diagonal] + [
            self.over_bit(b) for b in range(self.nbits)
        ]

    def barrier(self):
        sem = pltpu.get_barrier_semaphore()
        for peer in self.peers():
            pl.semaphore_signal(sem, inc=1, device_id=peer, device_id_type=MESH)
        pl.semaphore_wait(sem, 3 + self.nbits)


class Mover:
    def __init__(self, send, recv, local):
        self.send, self.recv, self.local_sems = send, recv, local
        self.n = self.m = 0
        self.sent = []

    def remote(self, src, dst, peer):
        one = pltpu.make_async_remote_copy(
            src_ref=src,
            dst_ref=dst,
            send_sem=self.send.at[self.n],
            recv_sem=self.recv.at[self.n],
            device_id=peer,
            device_id_type=MESH,
        )
        self.n += 1
        one.start()
        self.sent.append(one)
        return one

    def local(self, src, dst):
        one = pltpu.make_async_copy(src, dst, self.local_sems.at[self.m])
        self.m += 1
        one.start()
        return one

    def finish(self):
        for one in self.sent:
            one.wait_send()


def arrived(copies):
    for one in copies:
        one.wait_recv()


def pipe(body, grid, ins, outs):
    pltpu.emit_pipeline(
        body,
        grid=grid,
        in_specs=[
            pl.BlockSpec(v[1], v[2], pipeline_mode=pl.Buffered(1 if len(v) > 3 else 2)) for v in ins
        ],
        out_specs=[pl.BlockSpec(b, m) for _, b, m in outs],
    )(*[v[0] for v in ins], *[r for r, _, _ in outs])


def ds(start, size, step=None):
    return pl.ds(pl.multiple_of(start, step or size), size)


def normalize(x, sm, width):
    mean = jnp.mean(x, axis=1, keepdims=True)
    center = x - mean
    spread = jnp.mean(center * center, axis=1, keepdims=True)
    rstd = lax.rsqrt(spread + EPSILON)
    n = center * rstd
    one = (n * sm[:, pl.ds(0, width)] + sm[:, pl.ds(width, width)]).astype(BF)
    two = (n * sm[:, pl.ds(2 * width, width)] + sm[:, pl.ds(3 * width, width)]).astype(BF)
    lane = lax.broadcasted_iota(jnp.int32, (x.shape[0], 128), 1)
    return one, two, jnp.where(lane == 0, mean, rstd)


class Reduce:
    def __init__(self, me, mv, g, order, got, sums, ahead):
        self.me, self.mv, self.g, self.order = me, mv, g, order
        self.got, self.sums, self.ahead = got, sums, ahead
        self.step = 0
        self.flying = None
        self.fetched = []

    def at(self, level, step, last):
        gone = self.order[:level]
        out = []
        for b in range(self.me.nbits):
            if b in gone:
                continue
            if b in self.order[:step]:
                out.append(self.me.bits[b])
            elif step < len(self.order) and b == self.order[step]:
                out.append(last)
            else:
                out.append(slice(None))
        return tuple(out)

    def go(self):
        k = self.step
        if self.flying is not None:
            self.flying.wait_recv()
        b = self.order[k]
        other = 1 - self.me.bits[b]
        if k == 0:
            src = self.g.at[self.at(0, 0, other)]
        elif k == 1:
            src = self.sums[0]
            add_up([self.g.at[self.at(0, 1, other)], self.got[0].at[self.at(1, 1, other)]], src)
            for t in range(2, self.me.nbits + 1):
                last = 1 - self.me.bits[self.order[t]] if t < self.me.nbits else None
                for level, ref in ((0, self.g), (1, self.got[0])):
                    self.fetched.append(
                        self.mv.local(ref.at[self.at(level, t, last)], self.ahead[t - 2].at[level])
                    )
        else:
            src = self.sums[k - 1]
            self.total(k, other, src)
        self.flying = self.mv.remote(src, self.got[k], self.me.over_bit(b))
        self.step += 1

    def total(self, k, last, out):
        for one in self.fetched[2 * (k - 2) : 2 * (k - 1)]:
            one.wait()
        near = self.ahead[k - 2]
        later = [self.got[j - 1].at[self.at(j, k, last)] for j in range(2, k + 1)]
        lead = out.shape[:-2]
        rows = out.shape[-2]
        for m in range(2 ** len(lead)):
            at = tuple((m // 2 ** (len(lead) - 1 - i)) % 2 for i in range(len(lead)))
            value = near[(0,) + at].astype(F32) + near[(1,) + at].astype(F32)
            for one in later:
                value = value + one[at].astype(F32)
            out[at] = value.astype(out.dtype)

    def end(self, out):
        self.flying.wait_recv()
        self.total(self.me.nbits, None, out)


def add_up(sources, out):
    shape = sources[0].shape
    lead = shape[:-2]
    split = 2 if len(lead) < 2 else 1
    block = (1,) * len(lead) + (shape[-2] // split, shape[-1])

    def body(*refs):
        total = refs[0][...].astype(F32)
        for one in refs[1:-1]:
            total = total + one[...].astype(F32)
        refs[-1][...] = total.astype(refs[-1].dtype)

    index = lambda *g: g + (0,)
    pipe(body, lead + (split,), [(v, block, index) for v in sources], [(out, block, index)])


def attention_body(acc_k, acc_v, packed, gctx, tab, ctx_out, grad_out, sums):
    rows, width = gctx.shape[1:]
    t = tab[0]
    lane = lax.broadcasted_iota(jnp.int32, (rows, 128), 1)
    quart = ROT // 2
    cos = jnp.where(lane < quart, t, jnp.where(lane < ROT, pltpu.roll(t, quart, 1), 1.0))
    sin = jnp.where(lane < quart, -pltpu.roll(t, 128 - quart, 1), jnp.where(lane < ROT, t, 0.0))

    def rotate(v, at, sign):
        low = v[:, :128]
        swapped = jnp.where(
            lane[at] < quart, pltpu.roll(low, 128 - quart, 1), pltpu.roll(low, quart, 1)
        )
        return jnp.concatenate([low * cos[at] + swapped * (sign * sin[at]), v[:, 128:]], axis=1)

    ids_row = t.T[ROT : ROT + 1, :]
    inv_root = HEAD ** (-0.5)
    part = rows // 2
    every = slice(None)
    for h in range(width // HEAD):
        cq = pl.ds(h * HEAD, HEAD)
        ck = pl.ds(width + h * HEAD, HEAD)
        cv = pl.ds(2 * width + h * HEAD, HEAD)
        q = rotate(packed[0, :, cq], every, 1.0).astype(BF)
        k = rotate(packed[0, :, ck], every, 1.0).astype(BF)
        v = packed[0, :, cv].astype(BF)
        sum_q = None
        for p in range(2):
            at = slice(p * part, (p + 1) * part)
            keys = (p + 1) * part
            row = p * part + lax.broadcasted_iota(jnp.int32, (part, keys), 0)
            col = lax.broadcasted_iota(jnp.int32, (part, keys), 1)
            allowed = (t[at, ROT : ROT + 1] == ids_row[:, :keys]) & (col <= row)
            g = gctx[0, at, cq]
            scores = jnp.where(allowed, dot(q[at], k[:keys], 1, 1) * inv_root, NEG_FILL)
            peak = jnp.max(scores, axis=1, keepdims=True)
            e = jnp.exp(scores - peak)
            total = jnp.sum(e, axis=1, keepdims=True)
            probs = e * (1.0 / total)
            probs_b = probs.astype(BF)
            context = dot(probs_b, v[:keys], 1, 0)
            ctx_out[0, at, cq] = context.astype(BF)
            row_dot = jnp.sum(g.astype(F32) * context, axis=1, keepdims=True)
            grad_probs = dot(g, v[:keys], 1, 1)
            grad_scores = (probs * (grad_probs - row_dot) * inv_root).astype(BF)
            gq = rotate(dot(grad_scores, k[:keys], 1, 0), at, -1.0)
            grad_out[0, at, cq] = gq.astype(BF)
            one = jnp.sum(gq, axis=0, keepdims=True)
            sum_q = one if sum_q is None else sum_q + one
            gk = dot(grad_scores, q[at], 0, 0)
            gv = dot(probs_b, g, 0, 0)
            if p == 0:
                acc_k[:keys], acc_v[:keys] = gk, gv
            else:
                acc_k[:part] += gk[:part]
                acc_v[:part] += gv[:part]
                acc_k[part:keys], acc_v[part:keys] = gk[part:], gv[part:]
        gk = rotate(acc_k[...], every, -1.0)
        gv = acc_v[...]
        grad_out[0, :, ck] = gk.astype(BF)
        grad_out[0, :, cv] = gv.astype(BF)
        sums[0, :, cq] = jnp.broadcast_to(sum_q, (8, HEAD))
        sums[0, :, ck] = jnp.broadcast_to(jnp.sum(gk, axis=0, keepdims=True), (8, HEAD))
        sums[0, :, cv] = jnp.broadcast_to(jnp.sum(gv, axis=0, keepdims=True), (8, HEAD))


def gelu_and_slope(a):
    half_erf = 0.5 * lax.erf(a * 0.7071067811865476)
    cdf = 0.5 + half_erf
    slope = cdf + a * (jnp.exp(-0.5 * a * a) * 0.3989422804014327)
    return a * cdf, slope


def step_kernel(nbits, names, *refs):
    r = dict(zip(names, refs, strict=True))
    hid, cot, tab, small = r["hid"], r["cot"], r["tab"], r["small"]
    wqkv, wdense, wfc1, wfc2 = r["wqkv"], r["wdense"], r["wfc1"], r["wfc2"]
    xall, call, tall = r["xall"], r["call"], r["tall"]
    n1, n2, st = r["n1"], r["n2"], r["st"]
    gctx, gact, act, gpre, fsum = r["gctx"], r["gact"], r["act"], r["gpre"], r["fsum"]
    packed, ctx, gpk, qsum = r["packed"], r["ctx"], r["gpk"], r["qsum"]
    outp, outr, outx = r["outp"], r["outr"], r["outx"]
    up, ur, ux, usum = r["up"], r["ur"], r["ux"], r["usum"]
    wq, wf1, wf2, wd = r["wq"], r["wf1"], r["wf2"], r["wd"]
    sm_own, sm_got, sm = r["sm_own"], r["sm_got"], r["sm"]

    me = Place(nbits)
    s, c = me.s, me.c
    rows, width = hid.shape
    half = width // 2
    quarter = width // 4
    ffq = wf2.shape[0]
    mine = tuple(me.bits)
    every = (slice(None),) * (nbits + 1)
    mv = Mover(r["send"], r["recv"], r["lsem"])
    near, far = pl.ds(0, 2), pl.ds(2, 2)

    bring = [
        mv.local(small, sm_own),
        mv.local(wfc2.at[ds(c * ffq, ffq)], wf2),
        mv.local(wdense.at[ds(c * quarter, quarter)], wd),
    ]
    bring_w = [mv.local(wfc1.at[every + (ds((2 * s + c) * ffq, ffq),)], wf1.at[s])] + [
        mv.local(
            wqkv.at[every + (ds(g * width + (2 * s + c) * quarter, quarter),)],
            wq.at[(s,) + every + (pl.ds(g * quarter, quarter),)],
        )
        for g in range(3)
    ]
    me.barrier()

    away = 2 * (1 - s) + c
    x_small = mv.remote(small, sm_got, me.over_x)
    x_q = [
        mv.remote(
            wqkv.at[mine + (slice(None), ds(g * width + away * quarter, quarter))],
            wq.at[(s,) + mine + (slice(None), pl.ds(g * quarter, quarter))],
            me.over_x,
        )
        for g in range(3)
    ]
    x_f1 = mv.remote(
        wfc1.at[mine + (slice(None), ds(away * ffq, ffq))], wf1.at[(s,) + mine], me.over_x
    )
    c_cot = mv.remote(cot, call.at[1], me.over_core)
    c_hid = mv.remote(hid, xall.at[1], me.over_core)
    c_tab = mv.remote(tab, tall.at[1], me.over_core)

    last_bit = nbits - 1

    class Spread:
        def __init__(self, w, first):
            self.w, self.flying, self.final, self.b = w, first, [], 0

        def go(self):
            arrived(self.flying)
            self.flying = []
            b = self.b
            if b < last_bit:
                at = tuple(slice(None) if k < b else me.bits[k] for k in range(nbits))
                self.flying.append(
                    mv.remote(self.w.at[(1 - s,) + at], self.w.at[(1 - s,) + at], me.over_bit(b))
                )
            at = tuple(
                slice(None) if k < b - 1 else (1 - me.bits[k] if k == b - 1 else me.bits[k])
                for k in range(nbits)
            )
            self.final.append(
                mv.remote(self.w.at[(1 - s,) + at], self.w.at[(1 - s,) + at], me.over_bit(last_bit))
            )
            self.b += 1

        def done(self):
            while self.b <= last_bit:
                self.go()
            arrived(self.final)

    acc, got = r["acc"], r["got"]
    acc[0] = jnp.zeros(acc.shape[1:], F32)

    def stage(own_x, own_c, own_t):
        pairs = ((hid, own_x, xall.at[0]), (cot, own_c, call.at[0]), (tab, own_t, tall.at[0]))
        for one in [mv.local(a, b) for a, b, _ in pairs]:
            one.wait()
        out = [mv.local(b, o) for _, b, o in pairs]
        acc[0, 4:5, :] = jnp.sum(own_c[...].astype(F32), axis=0, keepdims=True)
        for one in out:
            one.wait()

    pl.run_scoped(
        stage,
        pltpu.VMEM((rows, width), BF),
        pltpu.VMEM((rows, width), BF),
        pltpu.VMEM((rows, 128), F32),
    )
    for one in bring:
        one.wait()

    tile = min(512, ffq)
    sub = rows // 2
    tok2 = lambda i, j: (i, j, 0)

    def from_cot(at):
        def body(a, o, ob):
            for k in range(ffq // tile):
                cols = pl.ds(k * tile, tile)
                o[0, :, cols] = dot(a[0], wf2[cols, :], 1, 1)
            ob[0] = dot(a[0], wd[...], 1, 1).astype(BF)

        pipe(
            body,
            (2, 2),
            [(call.at[at], (1, sub, width), tok2)],
            [(gact.at[at], (1, sub, ffq), tok2), (gctx.at[at], (1, sub, quarter), tok2)],
        )

    def from_cot_after(at):
        def body(a, slope, o, ob, o_sum):
            for k in range(ffq // tile):
                cols = pl.ds(k * tile, tile)
                grad = dot(a[0], wf2[cols, :], 1, 1) * slope[0, :, cols]
                o[0, :, cols] = grad.astype(BF)
                o_sum[0, :, cols] = jnp.broadcast_to(
                    jnp.sum(grad, axis=0, keepdims=True), (8, tile)
                )
            ob[0] = dot(a[0], wd[...], 1, 1).astype(BF)

        pipe(
            body,
            (2, 2),
            [(call.at[at], (1, sub, width), tok2), (gact.at[at], (1, sub, ffq), tok2)],
            [
                (gpre.at[at], (1, sub, ffq), tok2),
                (gctx.at[at], (1, sub, quarter), tok2),
                (fsum.at[at], (1, 8, ffq), tok2),
            ],
        )

    def norm_blocks(at):
        def body(x, o1, o2, ost):
            o1[0], o2[0], ost[0] = normalize(x[0].astype(F32), sm, width)

        pipe(
            body,
            (2, 2),
            [(xall.at[at], (1, sub, width), tok2)],
            [
                (n1.at[at], (1, sub, width), tok2),
                (n2.at[at], (1, sub, width), tok2),
                (st.at[at], (1, sub, 128), tok2),
            ],
        )

    bias_q = lambda g: sm[:, ds(4 * width + g * width + (2 * s + c) * quarter, quarter)]
    bias_f = lambda k: sm[:, ds(7 * width + (2 * s + c) * ffq + k * tile, tile)]
    all_rows = (slice(None),) + every

    def hidden_units(at):
        def body(a, g, o_act, o_pre, o_sum):
            for k in range(ffq // tile):
                cols = pl.ds(k * tile, tile)
                pre = dot(a[0], flat(wf1[all_rows + (cols,)]), 1, 0) + bias_f(k)
                value, slope = gelu_and_slope(pre)
                o_act[0, :, cols] = value.astype(BF)
                grad = g[0, :, cols] * slope
                o_pre[0, :, cols] = grad.astype(BF)
                o_sum[0, :, cols] = jnp.broadcast_to(
                    jnp.sum(grad, axis=0, keepdims=True), (8, tile)
                )

        pipe(
            body,
            (2, 2),
            [(n2.at[at], (1, sub, width), tok2), (gact.at[at], (1, sub, ffq), tok2)],
            [
                (act.at[at], (1, sub, ffq), tok2),
                (gpre.at[at], (1, sub, ffq), tok2),
                (fsum.at[at], (1, 8, ffq), tok2),
            ],
        )

    def forward(at):
        def body(one, two, o_act, o_slope, o_packed):
            for k in range(ffq // tile):
                cols = pl.ds(k * tile, tile)
                pre = dot(two[0], flat(wf1[all_rows + (cols,)]), 1, 0) + bias_f(k)
                value, slope = gelu_and_slope(pre)
                o_act[0, :, cols] = value.astype(BF)
                o_slope[0, :, cols] = slope
            for g in range(3):
                cols = pl.ds(g * quarter, quarter)
                o_packed[0, :, cols] = dot(one[0], flat(wq[all_rows + (cols,)]), 1, 0) + bias_q(g)

        pipe(
            body,
            (2, 2),
            [(n1.at[at], (1, sub, width), tok2), (n2.at[at], (1, sub, width), tok2)],
            [
                (act.at[at], (1, sub, ffq), tok2),
                (gact.at[at], (1, sub, ffq), tok2),
                (packed.at[at], (1, sub, 3 * quarter), tok2),
            ],
        )

    def project(at):
        def body(a, o):
            for g in range(3):
                cols = pl.ds(g * quarter, quarter)
                o[0, :, cols] = dot(a[0], flat(wq[all_rows + (cols,)]), 1, 0) + bias_q(g)

        pipe(
            body,
            (2, 2),
            [(n1.at[at], (1, sub, width), tok2)],
            [(packed.at[at], (1, sub, 3 * quarter), tok2)],
        )

    def attend(at):
        whole = lambda i: (i, 0, 0)
        pipe(
            partial(attention_body, r["acc_k"], r["acc_v"]),
            (2,),
            [
                (packed.at[at], (1, rows, 3 * quarter), whole),
                (gctx.at[at], (1, rows, quarter), whole),
                (tall.at[at], (1, rows, 128), whole),
            ],
            [
                (ctx.at[at], (1, rows, quarter), whole),
                (gpk.at[at], (1, rows, 3 * quarter), whole),
                (qsum.at[at], (1, 8, 3 * quarter), whole),
            ],
        )

    def finish(at, plus=None):
        def body(*refs):
            a, b, ga, gb, x, stat = refs[:6]
            o, ou, osum = refs[-3:]
            for k in range(4):
                cols = pl.ds(k * quarter, quarter)
                value = dot(a[0], wd[:, cols], 1, 0) + dot(b[0], wf2[:, cols], 1, 0)
                if plus is not None:
                    value = value + refs[6][0, :, cols].astype(F32)
                o[0, :, cols] = value.astype(BF)
            mean, rstd = stat[0, :, 0:1], stat[0, :, 1:2]
            for k in range(4):
                cols = pl.ds(k * quarter, quarter)
                one = dot(ga[0], flat(wq[k // 2, k % 2]), 1, 1)
                two = dot(gb[0], flat(wf1[k // 2, k % 2]), 1, 1)
                n = (x[0, :, cols].astype(F32) - mean) * rstd
                value = (
                    one * sm[:, pl.ds(k * quarter, quarter)]
                    + two * sm[:, pl.ds(2 * width + k * quarter, quarter)]
                )
                if plus is not None:
                    value = value + refs[7][0, :, cols].astype(F32)
                ou[0, :, cols] = value.astype(BF)
                osum[0, 0:1, cols] = jnp.sum(one * n, axis=0, keepdims=True)
                osum[0, 1:2, cols] = jnp.sum(one, axis=0, keepdims=True)
                osum[0, 2:3, cols] = jnp.sum(two * n, axis=0, keepdims=True)
                osum[0, 3:4, cols] = jnp.sum(two, axis=0, keepdims=True)

        pipe(
            body,
            (at.size, 2),
            [
                (ctx.at[at], (1, sub, quarter), tok2),
                (act.at[at], (1, sub, ffq), tok2),
                (gpk.at[at], (1, sub, 3 * quarter), tok2),
                (gpre.at[at], (1, sub, ffq), tok2),
                (xall.at[at], (1, sub, width), tok2),
                (st.at[at], (1, sub, 128), tok2),
            ]
            + [(v, (1, sub, width), tok2) for v in plus or ()],
            [
                (outp.at[at], (1, sub, width), tok2),
                (up.at[at], (1, sub, width), tok2),
                (usum.at[at], (1, 8, width), tok2),
            ],
        )

    def row_grad(lhs, keep, send, first, cols_tile, count):
        per_owner = keep.shape[-2]
        dims = keep.shape[:-2]
        lw = lhs.shape[2]

        def body(a, b, o_keep, o_send):
            full = dot(flat(a[...]), flat(b[...]), 0, 0).astype(BF)
            full = full.reshape((lw // (2 * per_owner), 2, per_owner, full.shape[-1]))
            zero, one = full[:, 0], full[:, 1]
            o_keep[...] = jnp.where(c == 0, zero, one).reshape(o_keep.shape)
            o_send[...] = jnp.where(c == 0, one, zero).reshape(o_send.shape)

        block = dims + (per_owner, cols_tile)
        at = lambda j: (0,) * (len(dims) + 1) + (j,)
        pipe(
            body,
            (count,),
            [
                (lhs, (4, rows, lw), lambda j: (0, 0, 0), True),
                (call, (4, rows, cols_tile), lambda j: (0, 0, first + j)),
            ],
            [(keep, block, at), (send, block, at)],
        )

    def column_grad(lhs, rhs, out, first):
        block = (1,) + out.shape[1:]

        def body(a, b, o):
            o[...] = dot(flat(a[...]), flat(b[...]), 0, 0).astype(BF).reshape(block)

        pipe(
            body,
            (2,),
            [
                (lhs, (4, rows, quarter), lambda j: (0, 0, first + j)),
                (rhs, (4, rows, rhs.shape[2]), lambda j: (0, 0, 0), True),
            ],
            [(out, block, lambda j: (j,) + (0,) * (len(block) - 1))],
        )

    usual = tuple(reversed(range(nbits)))
    swapped = (usual[1], usual[0]) + usual[2:] if nbits > 1 else usual

    def reduction(name, g, order):
        return Reduce(
            me,
            mv,
            g,
            order,
            [r[f"{name}_got{t}"] for t in range(nbits)],
            [r[f"{name}_sum{t}"] for t in range(1, nbits)],
            [r[f"{name}_ahead{t}"] for t in range(2, nbits + 1)],
        )

    f1 = Spread(wf1, [x_f1])
    q = Spread(wq, x_q)
    q.go()
    x_f1.wait_recv()
    f1.flying = []
    x_hid = mv.remote(hid, xall.at[2], me.over_x)
    c_cot.wait_recv()
    from_cot(near)
    x_small.wait_recv()
    lo = 0
    for n in (half, half, half, half, 3 * half, ffq * 2, half, half):
        sm[:, ds(2 * lo + s * n, n, 128)] = sm_own[:, pl.ds(lo, n)]
        sm[:, ds(2 * lo + (1 - s) * n, n, 128)] = sm_got[:, pl.ds(lo, n)]
        lo += n
    arrived([c_hid, c_tab])
    norm_blocks(near)
    q.go()
    f1.go()
    for one in bring_w:
        one.wait()
    for _ in range(2, nbits):
        q.go()
        f1.go()
    x_hid.wait_recv()
    d_hid = mv.remote(xall.at[2], xall.at[3], me.over_core)
    x_cot = mv.remote(cot, call.at[2], me.over_x)
    while f1.b <= last_bit:
        f1.go()
    d_hid.wait_recv()
    norm_blocks(far)
    q.done()
    project(near)
    attend(near)
    f1.done()
    hidden_units(near)
    x_cot.wait_recv()
    d_cot = mv.remote(call.at[2], call.at[3], me.over_core)
    x_tab = mv.remote(tab, tall.at[2], me.over_x)
    forward(far)
    d_cot.wait_recv()

    f2a, f2b, f2a_s, f2b_s = r["f2a"], r["f2b"], r["f2a_send"], r["f2b_send"]
    row_grad(act, f2a.at[c], f2a_s, 0, 512, width // 1024)
    f2a_swap = mv.remote(f2a_s, f2a.at[c], me.over_core)
    row_grad(act, f2b.at[c], f2b_s, width // 1024, 512, width // 1024)
    f2b_swap = mv.remote(f2b_s, f2b.at[c], me.over_core)
    f2a_swap.wait_recv()
    red_f2a = reduction("f2a", f2a, usual)
    red_f2a.go()
    x_tab.wait_recv()
    d_tab = mv.remote(tall.at[2], tall.at[3], me.over_core)
    from_cot_after(far)
    f2b_swap.wait_recv()
    red_f2b = reduction("f2b", f2b, usual)
    red_f2b.go()
    g1 = r["g1"]
    column_grad(n2, gpre, g1.at[0], 0)
    red_f1a = reduction("f1a", g1.at[0], swapped)
    red_f1a.go()
    column_grad(n2, gpre, g1.at[1], 2)
    red_f1b = reduction("f1b", g1.at[1], usual)
    red_f1b.go()

    d_tab.wait_recv()
    attend(far)
    red_f2a.go()
    gq = r["gq"]
    column_grad(n1, gpk, gq.at[0], 0)
    red_qa = reduction("qa", gq.at[0], usual)
    red_qa.go()
    column_grad(n1, gpk, gq.at[1], 2)
    red_qb = reduction("qb", gq.at[1], swapped)
    red_qb.go()
    red_f2b.go()
    d = r["d"]
    row_grad(ctx, d.at[c], r["d_send"], 0, 512, width // 512)
    d_swap = mv.remote(r["d_send"], d.at[c], me.over_core)
    red_f1a.go()
    d_swap.wait_recv()
    red_d = reduction("d", d, usual)
    red_d.go()

    finish(pl.ds(3, 1))
    o_far = mv.remote(outp.at[3], outr.at[1], me.over_core)
    u_far = mv.remote(up.at[3], ur.at[1], me.over_core)
    red_f1b.go()
    red_qb.go()
    red_f2a.go()
    arrived([o_far, u_far])
    finish(pl.ds(2, 1), (outr.at[pl.ds(1, 1)], ur.at[pl.ds(1, 1)]))
    o_x = mv.remote(outp.at[2], outx, me.over_x)
    u_x = mv.remote(up.at[2], ux, me.over_x)
    red_qa.go()
    red_d.go()
    red_f2b.go()
    red_f1a.go()
    finish(pl.ds(1, 1))
    u_near = mv.remote(up.at[1], ur.at[0], me.over_core)
    o_near = mv.remote(outp.at[1], outr.at[0], me.over_core)
    red_f1b.go()
    red_qb.go()
    red_qa.go()
    red_d.go()
    finish(pl.ds(0, 1))

    sums_in = [
        mv.local(usum, r["usum_v"]),
        mv.local(qsum, r["qsum_v"]),
        mv.local(fsum, r["fsum_v"]),
    ]
    for one in sums_in:
        one.wait()
    acc[0, 0:4, :] = jnp.sum(r["usum_v"][:, 0:4, :] + r["usum_v"][:, 8:12, :], axis=0)
    for g in range(3):
        acc[0, 5 + g : 6 + g, ds((2 * s + c) * quarter, quarter)] = jnp.sum(
            r["qsum_v"][:, 0:1, pl.ds(g * quarter, quarter)], axis=0
        )
    f_row = jnp.sum(r["fsum_v"][:, 0:1, :] + r["fsum_v"][:, 8:9, :], axis=0)
    acc[0, 8:9, ds(c * ffq, ffq)] = jnp.where(s == 0, f_row, 0.0)
    acc[0, 9:10, ds(c * ffq, ffq)] = jnp.where(s == 0, 0.0, f_row)
    small_peers = [me.over_x, me.over_core] + [me.over_bit(b) for b in range(nbits)]
    small_step = [0, None]

    def small_go():
        k, flying = small_step
        if k > len(small_peers):
            return
        if flying is not None:
            flying.wait_recv()
            acc[k] = acc[k - 1] + got[k - 1]
        if k < len(small_peers):
            small_step[1] = mv.remote(acc.at[k], got.at[k], small_peers[k])
        else:
            r["tot"][...] = acc[k]
        small_step[0] = k + 1

    small_go()
    reds = (red_f2a, red_f2b, red_f1a, red_f1b, red_qa, red_d, red_qb)
    for _ in range(nbits):
        for one in reds:
            if one.step < nbits:
                one.go()
                small_go()

    tok = lambda i: (i, 0)
    quarter_rows = rows // 4
    o_near.wait_recv()
    o_x.wait_recv()

    def result_body(x, a, b, e, o):
        o[...] = (
            x[...].astype(F32)
            + (
                a[...].astype(F32)
                + b[...].astype(F32)
                + e[...].astype(F32)
                + (sm[:, pl.ds(9 * width, width)] + sm[:, pl.ds(10 * width, width)])
            )
        ).astype(BF)

    block = (quarter_rows, width)
    pipe(
        result_body,
        (4,),
        [(v, block, tok) for v in (hid, outp.at[0], outr.at[0], outx)],
        [(r["result"], block, tok)],
    )
    u_near.wait_recv()
    u_x.wait_recv()

    def grad_body(x, y, a, b, e, stat, o):
        u = a[...].astype(F32) + b[...].astype(F32) + e[...].astype(F32)
        mean, rstd = stat[:, 0:1], stat[:, 1:2]
        n = (x[...].astype(F32) - mean) * rstd
        o[...] = y[...].astype(F32) + rstd * (
            u - jnp.mean(u, axis=1, keepdims=True) - n * jnp.mean(u * n, axis=1, keepdims=True)
        )

    pipe(
        grad_body,
        (4,),
        [(v, block, tok) for v in (hid, cot, up.at[0], ur.at[0], ux)]
        + [(st.at[0], (quarter_rows, 128), tok)],
        [(r["grad"], block, tok)],
    )
    small_go()

    last = []

    def hand_over(e, got):
        last.append(mv.remote(e.at[s, 1 - c], got.at[0], me.over_core))
        last.append(mv.remote(e.at[1 - s, c], got.at[1], me.over_x))
        last.append(mv.remote(e.at[1 - s, 1 - c], got.at[2], me.diagonal))

    e_f1, e_q, r_f1, r_q = r["e_f1"], r["e_q"], r["r_f1"], r["r_q"]
    for red, e, k, tmp in ((red_f1a, e_f1, 0, "end_f"), (red_f1b, e_f1, 1, "end_f")):
        red.end(r[tmp])
        e[k] = r[tmp][...].reshape(e.shape[1:])
    hand_over(e_f1, r_f1)
    red_f2a.end(r["o_f2"].at[:, pl.ds(0, half)])
    red_f2b.end(r["o_f2"].at[:, pl.ds(half, half)])
    red_d.end(r["o_d"])
    for red, e, k, tmp in ((red_qa, e_q, 0, "end_q"), (red_qb, e_q, 1, "end_q")):
        red.end(r[tmp])
        e[k] = r[tmp][...].reshape(e.shape[1:])
    hand_over(e_q, r_q)
    for _ in range(nbits + 3):
        small_go()
    arrived(last)
    places = ((s, c), (s, 1 - c), (1 - s, c), (1 - s, 1 - c))
    for k, (ps, pc) in enumerate(places):
        part_f = e_f1[s, c] if k == 0 else r_f1[k - 1]
        r["o_f1"][:, ds((2 * ps + pc) * ffq, ffq)] = part_f.astype(F32)
        for g in range(3):
            cols = pl.ds(g * quarter, quarter)
            part_q = e_q[s, c, :, cols] if k == 0 else r_q[k - 1, :, cols]
            r["o_q"][:, ds(g * width + (2 * ps + pc) * quarter, quarter)] = part_q.astype(F32)
    mv.finish()


def step(nbits, hid, cot, tab, small, wqkv, wdense, wfc1, wfc2):
    rows, width = hid.shape
    half, ff = wfc1.shape
    quarter, ffq = width // 4, ff // 4
    groups = 2**nbits
    own_rows = half // groups
    half_own = own_rows // 2
    per_ff = ffq // groups
    length = small.shape[1]
    bits = (2,) * nbits
    hbm, vmem = pl.BlockSpec(memory_space=pl.ANY), pl.BlockSpec(memory_space=pltpu.VMEM)
    sds = jax.ShapeDtypeStruct
    outs = {
        "result": (hbm, (rows, width), BF),
        "grad": (hbm, (rows, width), F32),
        "o_f2": (vmem, (per_ff, width), F32),
        "o_d": (vmem, (half_own, width), F32),
        "o_f1": (vmem, (half_own, ff), F32),
        "o_q": (vmem, (half_own, 3 * width), F32),
        "tot": (vmem, (16, width), F32),
        "xall": (hbm, (4, rows, width), BF),
        "call": (hbm, (4, rows, width), BF),
        "tall": (hbm, (4, rows, 128), F32),
        "n1": (hbm, (4, rows, width), BF),
        "n2": (hbm, (4, rows, width), BF),
        "st": (hbm, (4, rows, 128), F32),
        "gctx": (hbm, (4, rows, quarter), BF),
        "gact": (hbm, (4, rows, ffq), F32),
        "act": (hbm, (4, rows, ffq), BF),
        "gpre": (hbm, (4, rows, ffq), BF),
        "fsum": (hbm, (4, 16, ffq), F32),
        "packed": (hbm, (4, rows, 3 * quarter), F32),
        "ctx": (hbm, (4, rows, quarter), BF),
        "gpk": (hbm, (4, rows, 3 * quarter), BF),
        "qsum": (hbm, (4, 8, 3 * quarter), F32),
        "f2a": (hbm, bits + (per_ff, half), BF),
        "f2b": (hbm, bits + (per_ff, half), BF),
        "f2a_send": (hbm, bits[1:] + (per_ff, half), BF),
        "f2b_send": (hbm, bits[1:] + (per_ff, half), BF),
        "g1": (hbm, (2,) + bits + (own_rows, ffq), BF),
        "d": (hbm, bits + (half_own, width), BF),
        "d_send": (hbm, bits[1:] + (half_own, width), BF),
        "gq": (hbm, (2,) + bits + (own_rows, 3 * quarter), BF),
        "outp": (hbm, (4, rows, width), BF),
        "outr": (hbm, (2, rows, width), BF),
        "outx": (hbm, (rows, width), BF),
        "up": (hbm, (4, rows, width), BF),
        "ur": (hbm, (2, rows, width), BF),
        "ux": (hbm, (rows, width), BF),
        "usum": (hbm, (4, 16, width), F32),
    }
    extra = {}
    for name, tail in (
        ("f2a", (per_ff, half)),
        ("f2b", (per_ff, half)),
        ("f1a", (own_rows, ffq)),
        ("f1b", (own_rows, ffq)),
        ("d", (half_own, width)),
        ("qa", (own_rows, 3 * quarter)),
        ("qb", (own_rows, 3 * quarter)),
    ):
        for t in range(nbits):
            dims = (2,) * (nbits - 1 - t) + tail
            if t == 0:
                outs[f"{name}_got{t}"] = (hbm, dims, BF)
            else:
                extra[f"{name}_got{t}"] = pltpu.VMEM(dims, BF)
            if t == 1:
                outs[f"{name}_sum{t}"] = (hbm, dims, BF)
            if t > 1:
                extra[f"{name}_sum{t}"] = pltpu.VMEM(dims, BF)
        for t in range(2, nbits + 1):
            dims = (2,) * max(nbits - 1 - t, 0) + tail
            extra[f"{name}_ahead{t}"] = pltpu.VMEM((2,) + dims, BF)
    scratch = {
        "wq": pltpu.VMEM((2,) + bits + (own_rows, 3 * quarter), BF),
        "wf1": pltpu.VMEM((2,) + bits + (own_rows, ffq), BF),
        "wf2": pltpu.VMEM((ffq, width), BF),
        "wd": pltpu.VMEM((quarter, width), BF),
        "sm_own": pltpu.VMEM((1, length), F32),
        "sm_got": pltpu.VMEM((1, length), F32),
        "sm": pltpu.VMEM((1, 2 * length), F32),
        "acc_k": pltpu.VMEM((rows, HEAD), F32),
        "acc_v": pltpu.VMEM((rows, HEAD), F32),
        "usum_v": pltpu.VMEM((4, 16, width), F32),
        "qsum_v": pltpu.VMEM((4, 8, 3 * quarter), F32),
        "fsum_v": pltpu.VMEM((4, 16, ffq), F32),
        "acc": pltpu.VMEM((3 + nbits, 16, width), F32),
        "got": pltpu.VMEM((2 + nbits, 16, width), F32),
        "r_f1": pltpu.VMEM((3, half_own, ffq), BF),
        "r_q": pltpu.VMEM((3, half_own, 3 * quarter), BF),
        "e_f1": pltpu.VMEM((2, 2, half_own, ffq), BF),
        "e_q": pltpu.VMEM((2, 2, half_own, 3 * quarter), BF),
        "end_f": pltpu.VMEM((own_rows, ffq), BF),
        "end_q": pltpu.VMEM((own_rows, 3 * quarter), BF),
        "send": pltpu.SemaphoreType.DMA((36 + 12 * nbits,)),
        "recv": pltpu.SemaphoreType.DMA((36 + 12 * nbits,)),
        "lsem": pltpu.SemaphoreType.DMA((24 + 14 * nbits,)),
        **extra,
    }
    ins = ("hid", "cot", "tab", "small", "wqkv", "wdense", "wfc1", "wfc2")
    got = pl.pallas_call(
        partial(step_kernel, nbits, ins + tuple(outs) + tuple(scratch)),
        in_specs=[hbm] * len(ins),
        out_specs=[one[0] for one in outs.values()],
        out_shape=[sds(*one[1:]) for one in outs.values()],
        scratch_shapes=list(scratch.values()),
        compiler_params=pltpu.CompilerParams(
            collective_id=0, has_side_effects=True, vmem_limit_bytes=VMEM_LIMIT
        ),
        name="step",
    )(
        hid,
        cot,
        tab,
        small,
        wqkv.reshape(bits + (own_rows, 3 * width)),
        wdense,
        wfc1.reshape(bits + (own_rows, ff)),
        wfc2,
    )
    return got[:7]


def rotary_table(seg):
    rows = seg.shape[0]
    index = jnp.arange(rows, dtype=jnp.int32)
    same = seg[:, None] == seg[None, :]
    first = jnp.min(jnp.where(same, index[None, :], rows), axis=1)
    offset = (index - first).astype(F32)
    frequency = jnp.exp(-jnp.log(10000.0) * jnp.arange(0, ROT, 2).astype(F32) / ROT)
    angles = offset[:, None] * frequency[None, :]
    ids = jnp.broadcast_to(seg.astype(F32)[:, None], (rows, 128 - ROT))
    return jnp.concatenate([jnp.cos(angles), jnp.sin(angles), ids], axis=1)


def local(
    nbits,
    hidden_in,
    out_cotangent,
    segment_ids,
    ln1_gain,
    ln1_bias,
    qkv_weight,
    qkv_bias,
    dense_weight,
    dense_bias,
    ln2_gain,
    ln2_bias,
    fc1_weight,
    fc1_bias,
    fc2_weight,
    fc2_bias,
):
    me = lax.axis_index("shard") * 2 ** (nbits + 1) + lax.axis_index("replica")
    owners = 2 ** (nbits + 2)
    width = hidden_in.shape[1]
    vectors = (
        ln1_gain, ln1_bias, ln2_gain, ln2_bias, qkv_bias, fc1_bias, dense_bias, fc2_bias
    )
    length = sum(v.shape[0] for v in vectors)
    small, lo = 0.0, 0
    for v in vectors:
        n = v.shape[0]
        small = small + jnp.pad(v.astype(F32), (lo, length - lo - n))
        lo += n
    result, grad, o_f2, o_d, o_f1, o_q, tot = step(
        nbits,
        hidden_in,
        out_cotangent,
        rotary_table(segment_ids),
        small[None],
        qkv_weight,
        dense_weight,
        fc1_weight,
        fc2_weight,
    )

    def own(v):
        return lax.dynamic_index_in_dim(v.reshape(v.shape[:-1] + (owners, -1)), me, v.ndim - 1, False)

    five = own(tot[:5])
    b_qkv = own(tot[5:8].reshape(-1))
    b_fc1 = own(tot[8:10].reshape(-1))
    return (
        result, grad, five[0], five[1], o_q, b_qkv, o_d, five[4],
        five[2], five[3], o_f1, b_fc1, o_f2, five[4],
    )


def solution(mesh):
    both = ("shard", "replica")
    nbits = (mesh.shape["replica"] // 2).bit_length() - 1
    wide, token, vector, matrix = P(both, None), P(both), P("shard"), P("shard", None)
    return jax.shard_map(
        partial(local, nbits),
        mesh=mesh,
        in_specs=(wide, wide, token, vector, vector, matrix, vector, matrix, vector)
        + (vector, vector, matrix, vector, matrix, vector),
        out_specs=(wide, wide, token, token, wide, token, wide, token)
        + (token, token, wide, token, wide, token),
        check_vma=False,
    )
```

time: 2450 us -> 417 us (0.17)
  waiting for transfers between devices: 2060 us -> 0 us
  Pallas kernels: 0 us -> 392 us
  matrix products: 235 us -> 0 us
  other arithmetic: 44.3 us -> 5.05 us
  local copies, waits for them, and re-layouts: 51.9 us -> 14.8 us
  blocking collectives: 36.7 us -> 0 us
    reduce_scatter x4 -> x0, waiting for transfers between devices: 1340 us -> none  [the longest x1 440 us: local(): lax.psum_scatter(grad_w_qkv, ('shard', 'replica'), scatter_dimension=0, t...]
    all_gather x4 -> x0, waiting for transfers between devices: 705 us -> none  [the longest x1 259 us: local(): lax.all_gather(qkv_weight, 'shard', axis=0, tiled=True)]
    pallas_call x0 -> x1, Pallas kernels: none -> 392 us  [step(): pl.pallas_call(partial(step_kernel, nbits, ins + tuple(outs) + tuple(scra...]
    dot_general x18 -> x0, matrix products: 235 us -> none  [the longest x1 24.6 us: local(): jnp.einsum('td,tf->df', normed_one, grad_packed_b, preferred_element_type...]
    all_gather x8 -> x0, blocking collectives: 36.7 us -> none  [the longest x1 5.42 us: local(): lax.all_gather(ln1_gain, 'shard', axis=0, tiled=True)]
  transfers between devices with their start and end apart: 9 -> 0, of which waited for: 9 -> 0; matrix products, arithmetic and copies ran while one was open for 7% -> 0% of each run, Pallas kernels for 0% -> 0%
where the time goes in v1:
time: 417 us; the launch traced here: 413 us
  Pallas kernels  392 us (94%)
  local copies, waits for them, and re-layouts  14.8 us (4%)
  other arithmetic  5.05 us (1%)
    pallas_call x1, Pallas kernels, step(): pl.pallas_call(partial(step_kernel, nbits, ins + tuple(outs) + tuple(scra...  392 us
    unnamed x19, local copies, waits for them, and re-layouts  10.3 us

profile of v1, /device:TPU:0, one launch (start us, length us, event | category | flops | bytes accessed | tf_op | source)
XLA Modules:
  0.0 413.2 jit_solution(1358190621381289148)
XLA Ops:
  0.6 0.7 convert_element_type.43
  1.3 0.1 broadcast_in_dim.28
  1.5 1.0 select_reduce_fusion
  2.5 1.0 multiply_cosine_fusion
  3.5 0.9 pad_maximum_fusion.refs_2_
  4.4 1.4 convert_add_fusion
  5.8 392.4 %step.1 = (bf16[512,2048]{1,0:T(8,128)(2,1)}, f32[512,2048]{1,0:T(8,128)}, f32[128,2048]{1,0:T(8,128)}, f32[64,2048]{1,0:T(8,128)}, f32[64,4096]{1,0:T(8,128)}, ...) custom-call(bf16[512,2048]{1,0:T(8,128)(2,1)} %refs_0_.1, ...), custom_call_target="tpu_custom_call" | custom-call | tf_op jit(solution)/shard_map/step/pallas_call | solution.py:936
  398.3 0.8 slice.30
  399.1 0.1 reshape.66
  399.2 0.5 fusion
  399.7 0.8 slice.33
  400.6 0.1 reshape_reshape.6
  400.7 0.6 constant_dynamic-slice_fusion.5
  401.3 0.8 slice.37
  402.1 0.0 copy-start
  402.1 0.5 fusion.1
  402.7 0.5 copy.37
  403.2 3.4 copy.38
  406.6 2.1 copy.39
  408.7 0.4 copy-done.1
  409.1 1.1 copy.40
  410.2 0.8 copy.41
  411.0 1.0 copy.42
  412.0 1.0 copy.43
  (13 shorter events, 0.0 us)
Async XLA Ops:
  399.7 8.9 %copy-start.5 = (f32[64]{0:T(128)}, f32[64]{0:T(128)S(1)}, u32[]{:S(2)}) copy-start(f32[64]{0:T(128)S(1)} %get-tuple-element.84) | copy-start | bytes 772
  402.1 4.4 %copy-start = (f32[512,2048]{1,0:T(8,128)S(1)}, f32[512,2048]{1,0:T(8,128)}, u32[]{:S(2)}) copy-start(f32[512,2048]{1,0:T(8,128)} %get-tuple-element.78) | copy-start | bytes 12582916
  406.5 2.5 copy-start.1
  406.5 3.7 copy-start.4
  409.1 1.9 copy-start.3
  409.1 2.9 copy-start.2

commit v2 on v1

--- a/solution.py
+++ b/solution.py
@@ -16,7 +16,7 @@
 F32 = jnp.float32
 MESH = pl.DeviceIdType.MESH
 ANY = pl.BlockSpec(memory_space=pl.ANY)
-VMEM_LIMIT = 62 << 20
+VMEM_LIMIT = 127 << 19
 
 
 def dot(a, b, da, db):
@@ -117,10 +117,15 @@
     return one, two, jnp.where(lane == 0, mean, rstd)
 
 
+def blocks_of(shape):
+    lead = len(shape) - 2
+    return [tuple((m // 2 ** (lead - 1 - i)) % 2 for i in range(lead)) for m in range(2**lead)]
+
+
 class Reduce:
-    def __init__(self, me, mv, g, order, got, sums, ahead):
+    def __init__(self, me, mv, g, order, got, sums, ahead, came):
         self.me, self.mv, self.g, self.order = me, mv, g, order
-        self.got, self.sums, self.ahead = got, sums, ahead
+        self.got, self.sums, self.ahead, self.came = got, sums, ahead, came
         self.step = 0
         self.flying = None
         self.fetched = []
@@ -147,15 +152,22 @@
         other = 1 - self.me.bits[b]
         if k == 0:
             src = self.g.at[self.at(0, 0, other)]
+            if self.me.nbits > 1:
+                last = 1 - self.me.bits[self.order[1]]
+                self.first = self.mv.local(self.g.at[self.at(0, 1, last)], self.sums[0])
         elif k == 1:
             src = self.sums[0]
-            add_up([self.g.at[self.at(0, 1, other)], self.got[0].at[self.at(1, 1, other)]], src)
+            came = self.mv.local(self.got[0].at[self.at(1, 1, other)], self.came)
             for t in range(2, self.me.nbits + 1):
                 last = 1 - self.me.bits[self.order[t]] if t < self.me.nbits else None
                 for level, ref in ((0, self.g), (1, self.got[0])):
                     self.fetched.append(
                         self.mv.local(ref.at[self.at(level, t, last)], self.ahead[t - 2].at[level])
                     )
+            self.first.wait()
+            came.wait()
+            for at in blocks_of(src.shape):
+                src[at] = (src[at].astype(F32) + self.came[at].astype(F32)).astype(src.dtype)
         else:
             src = self.sums[k - 1]
             self.total(k, other, src)
@@ -167,10 +179,7 @@
             one.wait()
         near = self.ahead[k - 2]
         later = [self.got[j - 1].at[self.at(j, k, last)] for j in range(2, k + 1)]
-        lead = out.shape[:-2]
-        rows = out.shape[-2]
-        for m in range(2 ** len(lead)):
-            at = tuple((m // 2 ** (len(lead) - 1 - i)) % 2 for i in range(len(lead)))
+        for at in blocks_of(out.shape):
             value = near[(0,) + at].astype(F32) + near[(1,) + at].astype(F32)
             for one in later:
                 value = value + one[at].astype(F32)
@@ -181,23 +190,8 @@
         self.total(self.me.nbits, None, out)
 
 
-def add_up(sources, out):
-    shape = sources[0].shape
-    lead = shape[:-2]
-    split = 2 if len(lead) < 2 else 1
-    block = (1,) * len(lead) + (shape[-2] // split, shape[-1])
-
-    def body(*refs):
-        total = refs[0][...].astype(F32)
-        for one in refs[1:-1]:
-            total = total + one[...].astype(F32)
-        refs[-1][...] = total.astype(refs[-1].dtype)
-
-    index = lambda *g: g + (0,)
-    pipe(body, lead + (split,), [(v, block, index) for v in sources], [(out, block, index)])
-
-
-def attention_body(acc_k, acc_v, packed, gctx, tab, ctx_out, grad_out, sums):
+def attention_body(acc_k, acc_v, packed, project, normed, gctx, tab, ctx_out, grad_out, sums):
+    project(normed, packed)
     rows, width = gctx.shape[1:]
     t = tab[0]
     lane = lax.broadcasted_iota(jnp.int32, (rows, 128), 1)
@@ -216,22 +210,27 @@
     inv_root = HEAD ** (-0.5)
     part = rows // 2
     every = slice(None)
+    allowed = []
+    for p in range(2):
+        keys = (p + 1) * part
+        row = p * part + lax.broadcasted_iota(jnp.int32, (part, keys), 0)
+        col = lax.broadcasted_iota(jnp.int32, (part, keys), 1)
+        same = t[p * part : (p + 1) * part, ROT : ROT + 1] == ids_row[:, :keys]
+        allowed.append(same & (col <= row))
     for h in range(width // HEAD):
         cq = pl.ds(h * HEAD, HEAD)
         ck = pl.ds(width + h * HEAD, HEAD)
         cv = pl.ds(2 * width + h * HEAD, HEAD)
-        q = rotate(packed[0, :, cq], every, 1.0).astype(BF)
-        k = rotate(packed[0, :, ck], every, 1.0).astype(BF)
-        v = packed[0, :, cv].astype(BF)
+        q = (rotate(packed[:, cq], every, 1.0) * inv_root).astype(BF)
+        k = rotate(packed[:, ck], every, 1.0).astype(BF)
+        k_scaled = (k.astype(F32) * inv_root).astype(BF)
+        v = packed[:, cv].astype(BF)
         sum_q = None
         for p in range(2):
             at = slice(p * part, (p + 1) * part)
             keys = (p + 1) * part
-            row = p * part + lax.broadcasted_iota(jnp.int32, (part, keys), 0)
-            col = lax.broadcasted_iota(jnp.int32, (part, keys), 1)
-            allowed = (t[at, ROT : ROT + 1] == ids_row[:, :keys]) & (col <= row)
             g = gctx[0, at, cq]
-            scores = jnp.where(allowed, dot(q[at], k[:keys], 1, 1) * inv_root, NEG_FILL)
+            scores = jnp.where(allowed[p], dot(q[at], k[:keys], 1, 1), NEG_FILL)
             peak = jnp.max(scores, axis=1, keepdims=True)
             e = jnp.exp(scores - peak)
             total = jnp.sum(e, axis=1, keepdims=True)
@@ -241,8 +240,8 @@
             ctx_out[0, at, cq] = context.astype(BF)
             row_dot = jnp.sum(g.astype(F32) * context, axis=1, keepdims=True)
             grad_probs = dot(g, v[:keys], 1, 1)
-            grad_scores = (probs * (grad_probs - row_dot) * inv_root).astype(BF)
-            gq = rotate(dot(grad_scores, k[:keys], 1, 0), at, -1.0)
+            grad_scores = (probs * (grad_probs - row_dot)).astype(BF)
+            gq = rotate(dot(grad_scores, k_scaled[:keys], 1, 0), at, -1.0)
             grad_out[0, at, cq] = gq.astype(BF)
             one = jnp.sum(gq, axis=0, keepdims=True)
             sum_q = one if sum_q is None else sum_q + one
@@ -277,7 +276,7 @@
     xall, call, tall = r["xall"], r["call"], r["tall"]
     n1, n2, st = r["n1"], r["n2"], r["st"]
     gctx, gact, act, gpre, fsum = r["gctx"], r["gact"], r["act"], r["gpre"], r["fsum"]
-    packed, ctx, gpk, qsum = r["packed"], r["ctx"], r["gpk"], r["qsum"]
+    ctx, gpk, qsum = r["ctx"], r["gpk"], r["qsum"]
     outp, outr, outx = r["outp"], r["outr"], r["outx"]
     up, ur, ux, usum = r["up"], r["ur"], r["ux"], r["usum"]
     wq, wf1, wf2, wd = r["wq"], r["wf1"], r["wf2"], r["wd"]
@@ -321,6 +320,8 @@
     x_f1 = mv.remote(
         wfc1.at[mine + (slice(None), ds(away * ffq, ffq))], wf1.at[(s,) + mine], me.over_x
     )
+    x_hid = mv.remote(hid, xall.at[2], me.over_x)
+    x_cot = mv.remote(cot, call.at[2], me.over_x)
     c_cot = mv.remote(cot, call.at[1], me.over_core)
     c_hid = mv.remote(hid, xall.at[1], me.over_core)
     c_tab = mv.remote(tab, tall.at[1], me.over_core)
@@ -459,48 +460,33 @@
         )
 
     def forward(at):
-        def body(one, two, o_act, o_slope, o_packed):
+        def body(two, o_act, o_slope):
             for k in range(ffq // tile):
                 cols = pl.ds(k * tile, tile)
                 pre = dot(two[0], flat(wf1[all_rows + (cols,)]), 1, 0) + bias_f(k)
                 value, slope = gelu_and_slope(pre)
                 o_act[0, :, cols] = value.astype(BF)
                 o_slope[0, :, cols] = slope
-            for g in range(3):
-                cols = pl.ds(g * quarter, quarter)
-                o_packed[0, :, cols] = dot(one[0], flat(wq[all_rows + (cols,)]), 1, 0) + bias_q(g)
 
         pipe(
             body,
             (2, 2),
-            [(n1.at[at], (1, sub, width), tok2), (n2.at[at], (1, sub, width), tok2)],
-            [
-                (act.at[at], (1, sub, ffq), tok2),
-                (gact.at[at], (1, sub, ffq), tok2),
-                (packed.at[at], (1, sub, 3 * quarter), tok2),
-            ],
-        )
-
-    def project(at):
-        def body(a, o):
-            for g in range(3):
-                cols = pl.ds(g * quarter, quarter)
-                o[0, :, cols] = dot(a[0], flat(wq[all_rows + (cols,)]), 1, 0) + bias_q(g)
-
-        pipe(
-            body,
-            (2, 2),
-            [(n1.at[at], (1, sub, width), tok2)],
-            [(packed.at[at], (1, sub, 3 * quarter), tok2)],
-        )
+            [(n2.at[at], (1, sub, width), tok2)],
+            [(act.at[at], (1, sub, ffq), tok2), (gact.at[at], (1, sub, ffq), tok2)],
+        )
+
+    def project(a, o):
+        for g in range(3):
+            cols = pl.ds(g * quarter, quarter)
+            o[:, cols] = dot(a[0], flat(wq[all_rows + (cols,)]), 1, 0) + bias_q(g)
 
     def attend(at):
         whole = lambda i: (i, 0, 0)
         pipe(
-            partial(attention_body, r["acc_k"], r["acc_v"]),
+            partial(attention_body, r["acc_k"], r["acc_v"], r["packed"], project),
             (2,),
             [
-                (packed.at[at], (1, rows, 3 * quarter), whole),
+                (n1.at[at], (1, rows, width), whole),
                 (gctx.at[at], (1, rows, quarter), whole),
                 (tall.at[at], (1, rows, 128), whole),
             ],
@@ -511,16 +497,28 @@
             ],
         )
 
-    def finish(at, plus=None):
+    def finish(at, out=True, grad=True, plus=()):
+        more = list(plus)
+
         def body(*refs):
-            a, b, ga, gb, x, stat = refs[:6]
-            o, ou, osum = refs[-3:]
-            for k in range(4):
-                cols = pl.ds(k * quarter, quarter)
-                value = dot(a[0], wd[:, cols], 1, 0) + dot(b[0], wf2[:, cols], 1, 0)
-                if plus is not None:
-                    value = value + refs[6][0, :, cols].astype(F32)
-                o[0, :, cols] = value.astype(BF)
+            refs = list(refs)
+            take = lambda n: [refs.pop(0) for _ in range(n)]
+            if out:
+                a, b = take(2)
+            if grad:
+                ga, gb, x, stat = take(4)
+            extra = take(len(more))
+            if out:
+                o = refs.pop(0)
+                for k in range(4):
+                    cols = pl.ds(k * quarter, quarter)
+                    value = dot(a[0], wd[:, cols], 1, 0) + dot(b[0], wf2[:, cols], 1, 0)
+                    if more:
+                        value = value + extra[0][0, :, cols].astype(F32)
+                    o[0, :, cols] = value.astype(BF)
+            if not grad:
+                return
+            ou, osum = refs
             mean, rstd = stat[0, :, 0:1], stat[0, :, 1:2]
             for k in range(4):
                 cols = pl.ds(k * quarter, quarter)
@@ -531,32 +529,28 @@
                     one * sm[:, pl.ds(k * quarter, quarter)]
                     + two * sm[:, pl.ds(2 * width + k * quarter, quarter)]
                 )
-                if plus is not None:
-                    value = value + refs[7][0, :, cols].astype(F32)
+                if more:
+                    value = value + extra[-1][0, :, cols].astype(F32)
                 ou[0, :, cols] = value.astype(BF)
                 osum[0, 0:1, cols] = jnp.sum(one * n, axis=0, keepdims=True)
                 osum[0, 1:2, cols] = jnp.sum(one, axis=0, keepdims=True)
                 osum[0, 2:3, cols] = jnp.sum(two * n, axis=0, keepdims=True)
                 osum[0, 3:4, cols] = jnp.sum(two, axis=0, keepdims=True)
 
-        pipe(
-            body,
-            (at.size, 2),
-            [
-                (ctx.at[at], (1, sub, quarter), tok2),
-                (act.at[at], (1, sub, ffq), tok2),
+        ins, outs = [], []
+        if out:
+            ins += [(ctx.at[at], (1, sub, quarter), tok2), (act.at[at], (1, sub, ffq), tok2)]
+            outs += [(outp.at[at], (1, sub, width), tok2)]
+        if grad:
+            ins += [
                 (gpk.at[at], (1, sub, 3 * quarter), tok2),
                 (gpre.at[at], (1, sub, ffq), tok2),
                 (xall.at[at], (1, sub, width), tok2),
                 (st.at[at], (1, sub, 128), tok2),
             ]
-            + [(v, (1, sub, width), tok2) for v in plus or ()],
-            [
-                (outp.at[at], (1, sub, width), tok2),
-                (up.at[at], (1, sub, width), tok2),
-                (usum.at[at], (1, 8, width), tok2),
-            ],
-        )
+            outs += [(up.at[at], (1, sub, width), tok2), (usum.at[at], (1, 8, width), tok2)]
+        ins += [(v, (1, sub, width), tok2) for v in more]
+        pipe(body, (at.size, 2), ins, outs)
 
     def row_grad(lhs, keep, send, first, cols_tile, count):
         per_owner = keep.shape[-2]
@@ -582,26 +576,28 @@
             [(keep, block, at), (send, block, at)],
         )
 
-    def column_grad(lhs, rhs, out, first):
-        block = (1,) + out.shape[1:]
+    def column_grad(lhs, rhs, out, first, count):
+        block = (1, 1) + out.shape[2:]
 
         def body(a, b, o):
             o[...] = dot(flat(a[...]), flat(b[...]), 0, 0).astype(BF).reshape(block)
 
         pipe(
             body,
-            (2,),
+            (count,),
             [
                 (lhs, (4, rows, quarter), lambda j: (0, 0, first + j)),
                 (rhs, (4, rows, rhs.shape[2]), lambda j: (0, 0, 0), True),
             ],
-            [(out, block, lambda j: (j,) + (0,) * (len(block) - 1))],
+            [(out, block, lambda j: ((first + j) // 2, (first + j) % 2) + (0,) * (len(block) - 2))],
         )
 
     usual = tuple(reversed(range(nbits)))
-    swapped = (usual[1], usual[0]) + usual[2:] if nbits > 1 else usual
-
-    def reduction(name, g, order):
+
+    def order_of(name):
+        return tuple("hly".index(one) for one in name) if nbits == 3 else usual
+
+    def reduction(name, g, order, came):
         return Reduce(
             me,
             mv,
@@ -610,6 +606,7 @@
             [r[f"{name}_got{t}"] for t in range(nbits)],
             [r[f"{name}_sum{t}"] for t in range(1, nbits)],
             [r[f"{name}_ahead{t}"] for t in range(2, nbits + 1)],
+            r[came],
         )
 
     f1 = Spread(wf1, [x_f1])
@@ -617,7 +614,6 @@
     q.go()
     x_f1.wait_recv()
     f1.flying = []
-    x_hid = mv.remote(hid, xall.at[2], me.over_x)
     c_cot.wait_recv()
     from_cot(near)
     x_small.wait_recv()
@@ -637,13 +633,11 @@
         f1.go()
     x_hid.wait_recv()
     d_hid = mv.remote(xall.at[2], xall.at[3], me.over_core)
-    x_cot = mv.remote(cot, call.at[2], me.over_x)
     while f1.b <= last_bit:
         f1.go()
     d_hid.wait_recv()
     norm_blocks(far)
     q.done()
-    project(near)
     attend(near)
     f1.done()
     hidden_units(near)
@@ -654,85 +648,82 @@
     d_cot.wait_recv()
 
     f2a, f2b, f2a_s, f2b_s = r["f2a"], r["f2b"], r["f2a_send"], r["f2b_send"]
-    row_grad(act, f2a.at[c], f2a_s, 0, 512, width // 1024)
-    f2a_swap = mv.remote(f2a_s, f2a.at[c], me.over_core)
+    g1, gq, d = r["g1"], r["gq"], r["d"]
+    third, second = pl.ds(3, 1), pl.ds(2, 1)
     row_grad(act, f2b.at[c], f2b_s, width // 1024, 512, width // 1024)
     f2b_swap = mv.remote(f2b_s, f2b.at[c], me.over_core)
-    f2a_swap.wait_recv()
-    red_f2a = reduction("f2a", f2a, usual)
-    red_f2a.go()
     x_tab.wait_recv()
     d_tab = mv.remote(tall.at[2], tall.at[3], me.over_core)
     from_cot_after(far)
     f2b_swap.wait_recv()
-    red_f2b = reduction("f2b", f2b, usual)
+    red_f2b = reduction("f2b", f2b, order_of("lyh"), "came_f2")
     red_f2b.go()
-    g1 = r["g1"]
-    column_grad(n2, gpre, g1.at[0], 0)
-    red_f1a = reduction("f1a", g1.at[0], swapped)
+    column_grad(n2, gpre, g1, 2, 2)
+    red_f1b = reduction("f1b", g1.at[1], order_of("ylh"), "came_f1")
+    red_f1b.go()
+    column_grad(n2, gpre, g1, 0, 2)
+    red_f1a = reduction("f1a", g1.at[0], order_of("lhy"), "came_f1")
     red_f1a.go()
-    column_grad(n2, gpre, g1.at[1], 2)
-    red_f1b = reduction("f1b", g1.at[1], usual)
-    red_f1b.go()
-
     d_tab.wait_recv()
     attend(far)
-    red_f2a.go()
-    gq = r["gq"]
-    column_grad(n1, gpk, gq.at[0], 0)
-    red_qa = reduction("qa", gq.at[0], usual)
+    red_f1b.go()
+    red_f2b.go()
+    column_grad(n1, gpk, gq, 2, 2)
+    red_qb = reduction("q_b", gq.at[1], order_of("yhl"), "came_q_")
+    red_qb.go()
+    red_f1a.go()
+    column_grad(n1, gpk, gq, 0, 2)
+    red_qa = reduction("q_a", gq.at[0], order_of("lyh"), "came_q_")
     red_qa.go()
-    column_grad(n1, gpk, gq.at[1], 2)
-    red_qb = reduction("qb", gq.at[1], swapped)
-    red_qb.go()
     red_f2b.go()
-    d = r["d"]
+    finish(third, grad=False)
+    o_far = mv.remote(outp.at[3], outr.at[1], me.over_core)
+    red_f1b.go()
     row_grad(ctx, d.at[c], r["d_send"], 0, 512, width // 512)
     d_swap = mv.remote(r["d_send"], d.at[c], me.over_core)
+    o_far.wait_recv()
+    finish(second, grad=False, plus=(outr.at[pl.ds(1, 1)],))
+    o_x = mv.remote(outp.at[2], outx, me.over_x)
+    d_swap.wait_recv()
+    red_d = reduction("d", d, order_of("ylh"), "came_d")
+    red_d.go()
+    row_grad(act, f2a.at[c], f2a_s, 0, 512, width // 1024)
+    f2a_swap = mv.remote(f2a_s, f2a.at[c], me.over_core)
+    red_qb.go()
     red_f1a.go()
-    d_swap.wait_recv()
-    red_d = reduction("d", d, usual)
+    f2a_swap.wait_recv()
+    red_f2a = reduction("f2a", f2a, order_of("ylh"), "came_f2")
+    red_f2a.go()
+    finish(third, out=False)
+    u_far = mv.remote(up.at[3], ur.at[1], me.over_core)
     red_d.go()
-
-    finish(pl.ds(3, 1))
-    o_far = mv.remote(outp.at[3], outr.at[1], me.over_core)
-    u_far = mv.remote(up.at[3], ur.at[1], me.over_core)
-    red_f1b.go()
-    red_qb.go()
-    red_f2a.go()
-    arrived([o_far, u_far])
-    finish(pl.ds(2, 1), (outr.at[pl.ds(1, 1)], ur.at[pl.ds(1, 1)]))
-    o_x = mv.remote(outp.at[2], outx, me.over_x)
+    u_far.wait_recv()
+    finish(second, out=False, plus=(ur.at[pl.ds(1, 1)],))
     u_x = mv.remote(up.at[2], ux, me.over_x)
     red_qa.go()
-    red_d.go()
-    red_f2b.go()
-    red_f1a.go()
-    finish(pl.ds(1, 1))
+    finish(near)
     u_near = mv.remote(up.at[1], ur.at[0], me.over_core)
     o_near = mv.remote(outp.at[1], outr.at[0], me.over_core)
-    red_f1b.go()
-    red_qb.go()
-    red_qa.go()
-    red_d.go()
-    finish(pl.ds(0, 1))
-
-    sums_in = [
-        mv.local(usum, r["usum_v"]),
-        mv.local(qsum, r["qsum_v"]),
-        mv.local(fsum, r["fsum_v"]),
-    ]
-    for one in sums_in:
-        one.wait()
-    acc[0, 0:4, :] = jnp.sum(r["usum_v"][:, 0:4, :] + r["usum_v"][:, 8:12, :], axis=0)
-    for g in range(3):
-        acc[0, 5 + g : 6 + g, ds((2 * s + c) * quarter, quarter)] = jnp.sum(
-            r["qsum_v"][:, 0:1, pl.ds(g * quarter, quarter)], axis=0
-        )
-    f_row = jnp.sum(r["fsum_v"][:, 0:1, :] + r["fsum_v"][:, 8:9, :], axis=0)
-    acc[0, 8:9, ds(c * ffq, ffq)] = jnp.where(s == 0, f_row, 0.0)
-    acc[0, 9:10, ds(c * ffq, ffq)] = jnp.where(s == 0, 0.0, f_row)
-    small_peers = [me.over_x, me.over_core] + [me.over_bit(b) for b in range(nbits)]
+
+    def add_small(usum_v, qsum_v, fsum_v):
+        for one in [mv.local(usum, usum_v), mv.local(qsum, qsum_v), mv.local(fsum, fsum_v)]:
+            one.wait()
+        acc[0, 0:4, :] = jnp.sum(usum_v[:, 0:4, :] + usum_v[:, 8:12, :], axis=0)
+        for g in range(3):
+            acc[0, 5 + g : 6 + g, ds((2 * s + c) * quarter, quarter)] = jnp.sum(
+                qsum_v[:, 0:1, pl.ds(g * quarter, quarter)], axis=0
+            )
+        f_row = jnp.sum(fsum_v[:, 0:1, :] + fsum_v[:, 8:9, :], axis=0)
+        acc[0, 8:9, ds(c * ffq, ffq)] = jnp.where(s == 0, f_row, 0.0)
+        acc[0, 9:10, ds(c * ffq, ffq)] = jnp.where(s == 0, 0.0, f_row)
+
+    pl.run_scoped(
+        add_small,
+        pltpu.VMEM((4, 16, width), F32),
+        pltpu.VMEM((4, 8, 3 * quarter), F32),
+        pltpu.VMEM((4, 16, ffq), F32),
+    )
+    small_peers = [me.over_core] + [me.over_bit(b) for b in range(nbits)] + [me.over_x]
     small_step = [0, None]
 
     def small_go():
@@ -748,56 +739,42 @@
             r["tot"][...] = acc[k]
         small_step[0] = k + 1
 
+
     small_go()
-    reds = (red_f2a, red_f2b, red_f1a, red_f1b, red_qa, red_d, red_qb)
+    red_f2a.go()
+    small_go()
+    red_qa.go()
+    red_qb.go()
+    small_go()
+    red_d.go()
+    red_f2a.go()
+    small_go()
+
+
     for _ in range(nbits):
-        for one in reds:
+        for one in (red_f2a, red_f2b, red_f1a, red_f1b, red_qa, red_d, red_qb):
             if one.step < nbits:
                 one.go()
-                small_go()
-
     tok = lambda i: (i, 0)
-    quarter_rows = rows // 4
-    o_near.wait_recv()
-    o_x.wait_recv()
-
-    def result_body(x, a, b, e, o):
+    block = (rows // 8, width)
+
+    def result_body(x, y, a, b, e, ua, ub, ue, stat, o, ou):
+        xf = x[...].astype(F32)
         o[...] = (
-            x[...].astype(F32)
+            xf
             + (
                 a[...].astype(F32)
                 + b[...].astype(F32)
                 + e[...].astype(F32)
-                + (sm[:, pl.ds(9 * width, width)] + sm[:, pl.ds(10 * width, width)])
+                + (sm[:, pl.ds(7 * width + 4 * ffq, width)] + sm[:, pl.ds(8 * width + 4 * ffq, width)])
             )
         ).astype(BF)
-
-    block = (quarter_rows, width)
-    pipe(
-        result_body,
-        (4,),
-        [(v, block, tok) for v in (hid, outp.at[0], outr.at[0], outx)],
-        [(r["result"], block, tok)],
-    )
-    u_near.wait_recv()
-    u_x.wait_recv()
-
-    def grad_body(x, y, a, b, e, stat, o):
-        u = a[...].astype(F32) + b[...].astype(F32) + e[...].astype(F32)
+        u = ua[...].astype(F32) + ub[...].astype(F32) + ue[...].astype(F32)
         mean, rstd = stat[:, 0:1], stat[:, 1:2]
-        n = (x[...].astype(F32) - mean) * rstd
-        o[...] = y[...].astype(F32) + rstd * (
+        n = (xf - mean) * rstd
+        ou[...] = y[...].astype(F32) + rstd * (
             u - jnp.mean(u, axis=1, keepdims=True) - n * jnp.mean(u * n, axis=1, keepdims=True)
         )
-
-    pipe(
-        grad_body,
-        (4,),
-        [(v, block, tok) for v in (hid, cot, up.at[0], ur.at[0], ux)]
-        + [(st.at[0], (quarter_rows, 128), tok)],
-        [(r["grad"], block, tok)],
-    )
-    small_go()
 
     last = []
 
@@ -807,28 +784,63 @@
         last.append(mv.remote(e.at[1 - s, 1 - c], got.at[2], me.diagonal))
 
     e_f1, e_q, r_f1, r_q = r["e_f1"], r["e_q"], r["r_f1"], r["r_q"]
-    for red, e, k, tmp in ((red_f1a, e_f1, 0, "end_f"), (red_f1b, e_f1, 1, "end_f")):
-        red.end(r[tmp])
-        e[k] = r[tmp][...].reshape(e.shape[1:])
-    hand_over(e_f1, r_f1)
-    red_f2a.end(r["o_f2"].at[:, pl.ds(0, half)])
-    red_f2b.end(r["o_f2"].at[:, pl.ds(half, half)])
-    red_d.end(r["o_d"])
-    for red, e, k, tmp in ((red_qa, e_q, 0, "end_q"), (red_qb, e_q, 1, "end_q")):
-        red.end(r[tmp])
-        e[k] = r[tmp][...].reshape(e.shape[1:])
-    hand_over(e_q, r_q)
-    for _ in range(nbits + 3):
+
+    def owners(end_f, end_q, o_f1, o_q, o_f2, o_d):
+        before = len(mv.sent)
+        for k, red in enumerate((red_f1a, red_f1b)):
+            red.end(end_f)
+            e_f1[k] = end_f[...].reshape(e_f1.shape[1:])
+        hand_over(e_f1, r_f1)
+        for k, red in ((1, red_qb), (0, red_qa)):
+            red.end(end_q)
+            e_q[k] = end_q[...].reshape(e_q.shape[1:])
+        hand_over(e_q, r_q)
+        arrived([o_near, u_near, o_x, u_x])
         small_go()
-    arrived(last)
-    places = ((s, c), (s, 1 - c), (1 - s, c), (1 - s, 1 - c))
-    for k, (ps, pc) in enumerate(places):
-        part_f = e_f1[s, c] if k == 0 else r_f1[k - 1]
-        r["o_f1"][:, ds((2 * ps + pc) * ffq, ffq)] = part_f.astype(F32)
-        for g in range(3):
-            cols = pl.ds(g * quarter, quarter)
-            part_q = e_q[s, c, :, cols] if k == 0 else r_q[k - 1, :, cols]
-            r["o_q"][:, ds(g * width + (2 * ps + pc) * quarter, quarter)] = part_q.astype(F32)
+        pipe(
+            result_body,
+            (8,),
+            [
+                (v, block, tok)
+                for v in (hid, cot, outp.at[0], outr.at[0], outx, up.at[0], ur.at[0], ux)
+            ]
+            + [(st.at[0], (rows // 8, 128), tok)],
+            [(r["result"], block, tok), (r["grad"], block, tok)],
+        )
+        places = ((s, c), (s, 1 - c), (1 - s, c), (1 - s, 1 - c))
+        arrived(last)
+        for k, (ps, pc) in enumerate(places):
+            part = e_f1[s, c] if k == 0 else r_f1[k - 1]
+            o_f1[:, ds((2 * ps + pc) * ffq, ffq)] = part.astype(F32)
+        out = [mv.local(o_f1, r["o_f1"])]
+        for k, (ps, pc) in enumerate(places):
+            for g in range(3):
+                cols = pl.ds(g * quarter, quarter)
+                part = e_q[s, c, :, cols] if k == 0 else r_q[k - 1, :, cols]
+                o_q[:, ds(g * width + (2 * ps + pc) * quarter, quarter)] = part.astype(F32)
+        out.append(mv.local(o_q, r["o_q"]))
+        for _ in range(nbits + 3):
+            small_go()
+        red_f2b.end(o_f2.at[:, pl.ds(half, half)])
+        red_d.end(o_d)
+        out.append(mv.local(o_d, r["o_d"]))
+        red_f2a.end(o_f2.at[:, pl.ds(0, half)])
+        out.append(mv.local(o_f2, r["o_f2"]))
+        for one in out:
+            one.wait()
+        for one in mv.sent[before:]:
+            one.wait_send()
+        del mv.sent[before:]
+
+    pl.run_scoped(
+        owners,
+        pltpu.VMEM(g1.shape[-2:], BF),
+        pltpu.VMEM(gq.shape[-2:], BF),
+        pltpu.VMEM(r["o_f1"].shape, F32),
+        pltpu.VMEM(r["o_q"].shape, F32),
+        pltpu.VMEM(r["o_f2"].shape, F32),
+        pltpu.VMEM(r["o_d"].shape, F32),
+    )
     mv.finish()
 
 
@@ -847,10 +859,10 @@
     outs = {
         "result": (hbm, (rows, width), BF),
         "grad": (hbm, (rows, width), F32),
-        "o_f2": (vmem, (per_ff, width), F32),
-        "o_d": (vmem, (half_own, width), F32),
-        "o_f1": (vmem, (half_own, ff), F32),
-        "o_q": (vmem, (half_own, 3 * width), F32),
+        "o_f2": (hbm, (per_ff, width), F32),
+        "o_d": (hbm, (half_own, width), F32),
+        "o_f1": (hbm, (half_own, ff), F32),
+        "o_q": (hbm, (half_own, 3 * width), F32),
         "tot": (vmem, (16, width), F32),
         "xall": (hbm, (4, rows, width), BF),
         "call": (hbm, (4, rows, width), BF),
@@ -863,7 +875,6 @@
         "act": (hbm, (4, rows, ffq), BF),
         "gpre": (hbm, (4, rows, ffq), BF),
         "fsum": (hbm, (4, 16, ffq), F32),
-        "packed": (hbm, (4, rows, 3 * quarter), F32),
         "ctx": (hbm, (4, rows, quarter), BF),
         "gpk": (hbm, (4, rows, 3 * quarter), BF),
         "qsum": (hbm, (4, 8, 3 * quarter), F32),
@@ -890,8 +901,8 @@
         ("f1a", (own_rows, ffq)),
         ("f1b", (own_rows, ffq)),
         ("d", (half_own, width)),
-        ("qa", (own_rows, 3 * quarter)),
-        ("qb", (own_rows, 3 * quarter)),
+        ("q_a", (own_rows, 3 * quarter)),
+        ("q_b", (own_rows, 3 * quarter)),
     ):
         for t in range(nbits):
             dims = (2,) * (nbits - 1 - t) + tail
@@ -900,8 +911,8 @@
             else:
                 extra[f"{name}_got{t}"] = pltpu.VMEM(dims, BF)
             if t == 1:
-                outs[f"{name}_sum{t}"] = (hbm, dims, BF)
-            if t > 1:
+                extra[f"came_{name[:2]}"] = pltpu.VMEM(dims, BF)
+            if t > 0:
                 extra[f"{name}_sum{t}"] = pltpu.VMEM(dims, BF)
         for t in range(2, nbits + 1):
             dims = (2,) * max(nbits - 1 - t, 0) + tail
@@ -914,22 +925,18 @@
         "sm_own": pltpu.VMEM((1, length), F32),
         "sm_got": pltpu.VMEM((1, length), F32),
         "sm": pltpu.VMEM((1, 2 * length), F32),
+        "packed": pltpu.VMEM((rows, 3 * quarter), F32),
         "acc_k": pltpu.VMEM((rows, HEAD), F32),
         "acc_v": pltpu.VMEM((rows, HEAD), F32),
-        "usum_v": pltpu.VMEM((4, 16, width), F32),
-        "qsum_v": pltpu.VMEM((4, 8, 3 * quarter), F32),
-        "fsum_v": pltpu.VMEM((4, 16, ffq), F32),
         "acc": pltpu.VMEM((3 + nbits, 16, width), F32),
         "got": pltpu.VMEM((2 + nbits, 16, width), F32),
         "r_f1": pltpu.VMEM((3, half_own, ffq), BF),
         "r_q": pltpu.VMEM((3, half_own, 3 * quarter), BF),
         "e_f1": pltpu.VMEM((2, 2, half_own, ffq), BF),
         "e_q": pltpu.VMEM((2, 2, half_own, 3 * quarter), BF),
-        "end_f": pltpu.VMEM((own_rows, ffq), BF),
-        "end_q": pltpu.VMEM((own_rows, 3 * quarter), BF),
         "send": pltpu.SemaphoreType.DMA((36 + 12 * nbits,)),
         "recv": pltpu.SemaphoreType.DMA((36 + 12 * nbits,)),
-        "lsem": pltpu.SemaphoreType.DMA((24 + 14 * nbits,)),
+        "lsem": pltpu.SemaphoreType.DMA((40 + 14 * nbits,)),
         **extra,
     }
     ins = ("hid", "cot", "tab", "small", "wqkv", "wdense", "wfc1", "wfc2")

time: 417 us -> 376 us (0.902)
  Pallas kernels: 392 us -> 351 us
    pallas_call x1, Pallas kernels: 392 us -> 351 us  [step(): pl.pallas_call(partial(step_kernel, nbits, ins + tuple(outs) + tuple(scra...]
where the time goes in v2:
time: 376 us; the launch traced here: 372 us
  Pallas kernels  351 us (93%)
  local copies, waits for them, and re-layouts  14.8 us (4%)
  other arithmetic  5.05 us (1%)
    pallas_call x1, Pallas kernels, step(): pl.pallas_call(partial(step_kernel, nbits, ins + tuple(outs) + tuple(scra...  351 us
    unnamed x19, local copies, waits for them, and re-layouts  10.3 us

profile of v2, /device:TPU:0, one launch (start us, length us, event | category | flops | bytes accessed | tf_op | source)
XLA Modules:
  0.0 371.7 jit_solution(15847717614411346685)
XLA Ops:
  0.6 0.7 convert_element_type.43
  1.3 0.1 broadcast_in_dim.28
  1.5 1.0 select_reduce_fusion
  2.5 1.0 multiply_cosine_fusion
  3.5 0.9 pad_maximum_fusion.refs_2_
  4.4 1.4 convert_add_fusion
  5.8 350.9 %step.1 = (bf16[512,2048]{1,0:T(8,128)(2,1)}, f32[512,2048]{1,0:T(8,128)}, f32[128,2048]{1,0:T(8,128)}, f32[64,2048]{1,0:T(8,128)}, f32[64,4096]{1,0:T(8,128)}, ...) custom-call(bf16[512,2048]{1,0:T(8,128)(2,1)} %refs_0_.1, ...), custom_call_target="tpu_custom_call" | custom-call | tf_op jit(solution)/shard_map/step/pallas_call | solution.py:943
  356.8 0.8 slice.30
  357.6 0.1 reshape.66
  357.7 0.5 fusion
  358.2 0.8 slice.33
  359.1 0.1 reshape_reshape.6
  359.2 0.6 constant_dynamic-slice_fusion.5
  359.8 0.8 slice.37
  360.6 0.0 copy-start
  360.6 0.5 fusion.1
  361.2 0.5 copy.37
  361.7 3.4 copy.38
  365.1 2.1 copy.39
  367.2 0.4 copy-done.1
  367.6 1.1 copy.40
  368.7 0.8 copy.41
  369.5 1.0 copy.42
  370.5 1.0 copy.43
  (13 shorter events, 0.0 us)
Async XLA Ops:
  358.2 8.9 %copy-start.5 = (f32[64]{0:T(128)}, f32[64]{0:T(128)S(1)}, u32[]{:S(2)}) copy-start(f32[64]{0:T(128)S(1)} %get-tuple-element.84) | copy-start | bytes 772
  360.6 4.4 %copy-start = (f32[512,2048]{1,0:T(8,128)S(1)}, f32[512,2048]{1,0:T(8,128)}, u32[]{:S(2)}) copy-start(f32[512,2048]{1,0:T(8,128)} %get-tuple-element.78) | copy-start | bytes 12582916
  365.1 2.5 copy-start.1
  365.1 3.7 copy-start.4
  367.6 1.9 copy-start.3
  367.6 2.9 copy-start.2

commit v3 on v2

--- a/solution.py
+++ b/solution.py
@@ -704,6 +704,8 @@
     finish(near)
     u_near = mv.remote(up.at[1], ur.at[0], me.over_core)
     o_near = mv.remote(outp.at[1], outr.at[0], me.over_core)
+    red_f2a.go()
+    red_qb.go()
 
     def add_small(usum_v, qsum_v, fsum_v):
         for one in [mv.local(usum, usum_v), mv.local(qsum, qsum_v), mv.local(fsum, fsum_v)]:
@@ -723,7 +725,8 @@
         pltpu.VMEM((4, 8, 3 * quarter), F32),
         pltpu.VMEM((4, 16, ffq), F32),
     )
-    small_peers = [me.over_core] + [me.over_bit(b) for b in range(nbits)] + [me.over_x]
+    bits_in_turn = (0,) + tuple(reversed(range(1, nbits)))
+    small_peers = [me.over_core] + [me.over_bit(b) for b in bits_in_turn] + [me.over_x]
     small_step = [0, None]
 
     def small_go():
@@ -741,14 +744,10 @@
 
 
     small_go()
-    red_f2a.go()
-    small_go()
     red_qa.go()
-    red_qb.go()
     small_go()
     red_d.go()
     red_f2a.go()
-    small_go()
 
 
     for _ in range(nbits):
@@ -791,12 +790,7 @@
             red.end(end_f)
             e_f1[k] = end_f[...].reshape(e_f1.shape[1:])
         hand_over(e_f1, r_f1)
-        for k, red in ((1, red_qb), (0, red_qa)):
-            red.end(end_q)
-            e_q[k] = end_q[...].reshape(e_q.shape[1:])
-        hand_over(e_q, r_q)
         arrived([o_near, u_near, o_x, u_x])
-        small_go()
         pipe(
             result_body,
             (8,),
@@ -807,12 +801,25 @@
             + [(st.at[0], (rows // 8, 128), tok)],
             [(r["result"], block, tok), (r["grad"], block, tok)],
         )
+        small_go()
+        for k, red in ((1, red_qb), (0, red_qa)):
+            red.end(end_q)
+            e_q[k] = end_q[...].reshape(e_q.shape[1:])
+        hand_over(e_q, r_q)
+        small_go()
         places = ((s, c), (s, 1 - c), (1 - s, c), (1 - s, 1 - c))
-        arrived(last)
+        arrived(last[:3])
         for k, (ps, pc) in enumerate(places):
             part = e_f1[s, c] if k == 0 else r_f1[k - 1]
             o_f1[:, ds((2 * ps + pc) * ffq, ffq)] = part.astype(F32)
         out = [mv.local(o_f1, r["o_f1"])]
+        red_f2b.end(o_f2.at[:, pl.ds(half, half)])
+        red_d.end(o_d)
+        out.append(mv.local(o_d, r["o_d"]))
+        small_go()
+        red_f2a.end(o_f2.at[:, pl.ds(0, half)])
+        out.append(mv.local(o_f2, r["o_f2"]))
+        arrived(last[3:])
         for k, (ps, pc) in enumerate(places):
             for g in range(3):
                 cols = pl.ds(g * quarter, quarter)
@@ -821,11 +828,6 @@
         out.append(mv.local(o_q, r["o_q"]))
         for _ in range(nbits + 3):
             small_go()
-        red_f2b.end(o_f2.at[:, pl.ds(half, half)])
-        red_d.end(o_d)
-        out.append(mv.local(o_d, r["o_d"]))
-        red_f2a.end(o_f2.at[:, pl.ds(0, half)])
-        out.append(mv.local(o_f2, r["o_f2"]))
         for one in out:
             one.wait()
         for one in mv.sent[before:]:

time: 376 us -> 378 us (level)
  no operation moved by 1% of the time
where the time goes in v3:
time: 378 us; the launch traced here: 374 us
  Pallas kernels  353 us (93%)
  local copies, waits for them, and re-layouts  14.8 us (4%)
  other arithmetic  5.05 us (1%)
    pallas_call x1, Pallas kernels, step(): pl.pallas_call(partial(step_kernel, nbits, ins + tuple(outs) + tuple(scra...  353 us
    unnamed x19, local copies, waits for them, and re-layouts  10.3 us

profile of v3, /device:TPU:0, one launch (start us, length us, event | category | flops | bytes accessed | tf_op | source)
XLA Modules:
  0.0 373.6 jit_solution(723765572779054981)
XLA Ops:
  0.6 0.7 convert_element_type.43
  1.3 0.1 broadcast_in_dim.28
  1.5 1.0 select_reduce_fusion
  2.5 1.0 multiply_cosine_fusion
  3.5 0.9 pad_maximum_fusion.refs_2_
  4.4 1.4 convert_add_fusion
  5.8 352.9 %step.1 = (bf16[512,2048]{1,0:T(8,128)(2,1)}, f32[512,2048]{1,0:T(8,128)}, f32[128,2048]{1,0:T(8,128)}, f32[64,2048]{1,0:T(8,128)}, f32[64,4096]{1,0:T(8,128)}, ...) custom-call(bf16[512,2048]{1,0:T(8,128)(2,1)} %refs_0_.1, ...), custom_call_target="tpu_custom_call" | custom-call | tf_op jit(solution)/shard_map/step/pallas_call | solution.py:945
  358.7 0.8 slice.30
  359.6 0.1 reshape.66
  359.7 0.5 fusion
  360.2 0.8 slice.33
  361.1 0.1 reshape_reshape.6
  361.1 0.6 constant_dynamic-slice_fusion.5
  361.7 0.8 slice.37
  362.6 0.0 copy-start
  362.6 0.5 fusion.1
  363.1 0.5 copy.37
  363.6 3.4 copy.38
  367.0 2.1 copy.39
  369.1 0.4 copy-done.1
  369.6 1.1 copy.40
  370.7 0.8 copy.41
  371.5 1.0 copy.42
  372.5 1.0 copy.43
  (13 shorter events, 0.0 us)
Async XLA Ops:
  360.2 8.9 %copy-start.5 = (f32[64]{0:T(128)}, f32[64]{0:T(128)S(1)}, u32[]{:S(2)}) copy-start(f32[64]{0:T(128)S(1)} %get-tuple-element.84) | copy-start | bytes 772
  362.6 4.4 %copy-start = (f32[512,2048]{1,0:T(8,128)S(1)}, f32[512,2048]{1,0:T(8,128)}, u32[]{:S(2)}) copy-start(f32[512,2048]{1,0:T(8,128)} %get-tuple-element.78) | copy-start | bytes 12582916
  367.0 2.5 copy-start.1
  367.0 3.7 copy-start.4
  369.5 1.9 copy-start.3
  369.6 2.9 copy-start.2
